TPU v7x, 32 devices: a whole 2x2x4 slice. The times are simulated.
32 devices in a mesh: dp: 8 (over z, y), ep: 4 (over x, core).
Axes of the slice: x: 2, y: 2, z: 4, core: 2. Of those that a mesh axis runs over, the one named last changes fastest.
Arguments:
- x: bfloat16 [65536, 768], P(('dp', 'ep'))
- gy: bfloat16 [65536, 768], P(('dp', 'ep'))
- idx: int32 [65536], P(('dp', 'ep'))
- w_gate: bfloat16 [768, 8], replicated
- w_up: bfloat16 [8, 768, 3072], P('ep')
- w_down: bfloat16 [8, 3072, 768], P('ep')
Outputs:
- output 1: bfloat16 [65536, 768], P(('dp', 'ep'))
- output 2: bfloat16 [65536, 768], P(('dp', 'ep'))
- output 3: float32 [8, 768, 3072], P('ep')
- output 4: float32 [8, 3072, 768], P('ep')
- output 5: float32 [768, 8], replicated
All inputs are finite; a program needn't handle non-finite values.
Results may differ from a plain program's by a relative error of at most 0.00594816.
Values are sent between devices in bfloat16 or wider.
A program may use at most 1 GiB of HBM per device.

v0:
```python
import jax
import jax.numpy as jnp
from jax import lax
from jax.sharding import PartitionSpec as P

PAD_FACTOR = 4


def solution(mesh):
    ep_size = mesh.shape['ep']
    tok_spec = P(('dp', 'ep'), None)
    idx_spec = P(('dp', 'ep'))
    rep_spec = P(None, None)
    exp_spec = P('ep', None, None)

    def local_step(x_loc, gy_loc, idx_loc, w_gate, w_up, w_down):
        tok_count, d_model = x_loc.shape
        n_experts = w_gate.shape[1]
        local_experts = w_up.shape[0]
        cap_rows = PAD_FACTOR * tok_count // n_experts
        onehot = idx_loc[:, None] == jnp.arange(n_experts, dtype=jnp.int32)[None, :]
        expert_count = jnp.sum(onehot, axis=0, dtype=jnp.int32)
        sort_order = jnp.argsort(idx_loc, stable=True)
        sorted_pos = jnp.argsort(sort_order)
        expert_start = jnp.cumsum(expert_count) - expert_count
        slot_k = jnp.arange(cap_rows, dtype=jnp.int32)
        slot_valid = slot_k[None, :] < expert_count[:, None]
        src_tok = sort_order[jnp.minimum(expert_start[:, None] + slot_k[None, :], tok_count - 1)]
        slot_tok = idx_loc * cap_rows + sorted_pos - expert_start[idx_loc]

        def dispatch(tok_rows):
            picked = jnp.where(slot_valid[:, :, None], tok_rows[src_tok], jnp.zeros((), tok_rows.dtype))
            picked = picked.reshape(ep_size, local_experts, cap_rows, d_model)
            return lax.all_to_all(picked, 'ep', 0, 0, tiled=True)

        def combine(expert_rows):
            returned = lax.all_to_all(expert_rows, 'ep', 1, 0, tiled=True)
            return returned.reshape(n_experts * cap_rows, d_model)[slot_tok]

        router_logit = jnp.dot(x_loc, w_gate, preferred_element_type=jnp.float32)
        router_prob = jax.nn.softmax(router_logit, axis=-1)
        gate_val = n_experts * jnp.sum(jnp.where(onehot, router_prob, 0.0), axis=1)
        recv_rows = dispatch(x_loc)
        pre_act = jnp.einsum('sekd,edf->eskf', recv_rows, w_up, preferred_element_type=jnp.float32)
        hid_full, gelu_back = jax.vjp(jax.nn.gelu, pre_act)
        hidden = hid_full.astype(jnp.bfloat16)
        expert_out = jnp.einsum('eskf,efd->eskd', hidden, w_down, preferred_element_type=jnp.float32).astype(jnp.bfloat16)
        y_tok = combine(expert_out)
        gy_full = gy_loc.astype(jnp.float32)
        moe_out = (gate_val[:, None] * y_tok.astype(jnp.float32)).astype(jnp.bfloat16)

        dy_tok = (gate_val[:, None] * gy_full).astype(jnp.bfloat16)
        recv_grad = dispatch(dy_tok)
        d_hidden = jnp.einsum('sekd,efd->eskf', recv_grad, w_down, preferred_element_type=jnp.float32)
        d_pre = gelu_back(d_hidden)[0].astype(jnp.bfloat16)
        grad_down = jnp.einsum('eskf,sekd->efd', hidden, recv_grad, preferred_element_type=jnp.float32)
        grad_up = jnp.einsum('sekd,eskf->edf', recv_rows, d_pre, preferred_element_type=jnp.float32)
        d_rows = jnp.einsum('eskf,edf->eskd', d_pre, w_up, preferred_element_type=jnp.float32).astype(jnp.bfloat16)
        dx_expert = combine(d_rows)
        d_gate = jnp.sum(gy_full * y_tok.astype(jnp.float32), axis=1)
        d_logit = ((d_gate * gate_val)[:, None] * (onehot.astype(jnp.float32) - router_prob)).astype(jnp.bfloat16)
        dx_router = jnp.einsum('te,de->td', d_logit, w_gate, preferred_element_type=jnp.float32)
        grad_x = (dx_expert.astype(jnp.float32) + dx_router).astype(jnp.bfloat16)
        grad_gate = jnp.einsum('td,te->de', x_loc, d_logit, preferred_element_type=jnp.float32)
        grad_up = lax.psum(grad_up, 'dp')
        grad_down = lax.psum(grad_down, 'dp')
        grad_gate = lax.psum(grad_gate, ('dp', 'ep'))
        return moe_out, grad_x, grad_up, grad_down, grad_gate

    sharded_fn = jax.shard_map(local_step, mesh=mesh, in_specs=(tok_spec, tok_spec, idx_spec, rep_spec, exp_spec, exp_spec), out_specs=(tok_spec, tok_spec, exp_spec, exp_spec, rep_spec), check_vma=False)
    return sharded_fn
```

profile of v0, /device:TPU:0, one launch (start us, length us, event | category | flops | bytes accessed | tf_op | source)
XLA Modules:
  0.0 2071.6 jit_solution(10920020404056259954)
XLA Ops:
  7.2 1.0 convert_reduce_fusion
  8.4 5.7 sort.34
  14.3 45.5 %gather_fusion = s32[8192]{0:T(1024)S(1)} fusion(s32[2048]{0:T(1024)S(1)} %get-tuple-element.7, s32[8192]{0:T(1024)S(1)} %bitcast_clamp_fusion.1), kind=kCustom, calls=%fused_computation | custom fusion | bytes 98304 | tf_op jit(solution)/shard_map/gather | solution.py:28
  60.0 34.4 %gather_fusion.1 = bf16[8192,768]{1,0:T(8,128)(2,1)} fusion(bf16[2048,768]{1,0:T(8,128)(2,1)S(1)} %copy-done, s32[8192]{0:T(1024)S(1)} %bitcast_clamp_fusion), kind=kCustom, calls=%fused_computation.1 | custom fusion | bytes 25198592 | tf_op jit(solution)/shard_map/gather | solution.py:32
  94.5 6.9 broadcast_select_fusion.1
  101.4 143.1 %all_to_all.40 = bf16[4,2,1024,768]{3,2,1,0:T(8,128)(2,1)} all-to-all(bf16[4,2,1024,768]{3,2,1,0:T(8,128)(2,1)S(1)} %broadcast_select_fusion.1), channel_id=1, replica_groups=mesh['dp'=8,'ep'=4] {'ep'}, dimensions={0} | all-to-all | bytes 25165824 | tf_op jit(solution)/shard_map/all_to_all | solution.py:34
  244.5 70.2 %multiply_convert_fusion = (bf16[2,4,1024,3072]{3,2,1,0:T(8,128)(2,1)}, f32[2,4,1024,3072]{3,2,1,0:T(8,128)}) fusion(bf16[2,768,3072]{2,1,0:T(8,128)(2,1)} %param.10, bf16[4,2,1024,768]{3,2,1,0:T(8,128)(2,1)} %all_to_all.40), kind=kOutput, calls=%fused_computation.14 | convolution fusion | flops 38881198080 | bytes 173015040 | tf_op jit(solution)/shard_map/sekd,edf->eskf/dot_general | solution.py:44
  314.7 45.9 %fusion.26 = bf16[2,4,1024,768]{3,2,1,0:T(8,128)(2,1)S(1)} fusion(bf16[2,4,1024,3072]{3,2,1,0:T(8,128)(2,1)} %get-tuple-element.22, bf16[2,3072,768]{2,1,0:T(8,128)(2,1)} %param.11), kind=kOutput, calls=%fused_computation.35 | convolution fusion | flops 38660997120 | bytes 72351744 | tf_op jit(solution)/shard_map/eskf,efd->eskd/dot_general | solution.py:47
  360.6 5.1 copy.22
  365.6 6.5 all-to-all-start.1
  372.8 5.0 sort.35
  380.6 4.8 fusion.39
  385.5 124.7 %all-to-all-done.1 = bf16[2,4,1024,768]{3,2,0,1:T(8,128)(2,1)} async-done(((bf16[2,4,1024,768]{3,2,0,1:T(8,128)(2,1)}), bf16[2,4,1024,768]{3,2,0,1:T(8,128)(2,1)}, u32[]{:S(2)}, u32[]{:S(2)}) %all-to-all-start.1) | async-done | bytes 12582944 | tf_op jit(solution)/shard_map/all_to_all | solution.py:37
  510.2 16.3 gather_fusion.2
  526.4 6.0 fusion.34
  532.5 39.3 %gather_fusion.3 = bf16[8192,768]{1,0:T(8,128)(2,1)} fusion(bf16[2048,768]{1,0:T(8,128)(2,1)} %get-tuple-element.12, s32[8192]{0:T(1024)S(1)} %copy-done.8), kind=kCustom, calls=%fused_computation.3 | custom fusion | bytes 25198592 | tf_op jit(solution)/shard_map/gather | solution.py:32
  571.8 6.9 broadcast_select_fusion
  578.7 142.3 %all_to_all.41 = bf16[4,2,1024,768]{3,2,1,0:T(8,128)(2,1)} all-to-all(bf16[4,2,1024,768]{3,2,1,0:T(8,128)(2,1)S(1)} %broadcast_select_fusion), channel_id=1, replica_groups=mesh['dp'=8,'ep'=4] {'ep'}, dimensions={0} | all-to-all | bytes 25165824 | tf_op jit(solution)/shard_map/all_to_all | solution.py:34
  721.0 48.4 %fusion.20 = f32[2,3072,768]{2,1,0:T(8,128)} fusion(bf16[2,4,1024,3072]{3,2,1,0:T(8,128)(2,1)} %get-tuple-element.22, bf16[4,2,1024,768]{3,2,1,0:T(8,128)(2,1)} %all_to_all.41), kind=kOutput, calls=%fused_computation.30 | convolution fusion | flops 38654705664 | bytes 81788928 | tf_op jit(solution)/shard_map/eskf,sekd->efd/dot_general | solution.py:56
  769.4 98.3 %fusion.6 = bf16[2,4,1024,3072]{3,2,1,0:T(8,128)(2,1)} fusion(f32[2,4,1024,3072]{3,2,1,0:T(8,128)} %get-tuple-element.23, bf16[4,2,1024,768]{3,2,1,0:T(8,128)(2,1)} %all_to_all.41, bf16[2,3072,768]{2,1,0:T(8,128)(2,1)} %param.11), kind=kOutput, calls=%fused_computation.13 | convolution fusion | flops 39158022144 | bytes 173015040 | tf_op jit(solution)/shard_map/sekd,efd->eskf/dot_general | solution.py:54
  867.7 47.7 %fusion.23 = f32[2,768,3072]{2,1,0:T(8,128)} fusion(bf16[4,2,1024,768]{3,2,1,0:T(8,128)(2,1)} %all_to_all.40, bf16[2,4,1024,3072]{3,2,1,0:T(8,128)(2,1)} %fusion.6), kind=kOutput, calls=%fused_computation.31 | convolution fusion | flops 38654705664 | bytes 81788928 | tf_op jit(solution)/shard_map/sekd,eskf->edf/dot_general | solution.py:57
  915.4 47.3 %fusion.29 = bf16[2,4,1024,768]{3,2,1,0:T(8,128)(2,1)} fusion(bf16[2,4,1024,3072]{3,2,1,0:T(8,128)(2,1)} %fusion.6, bf16[2,768,3072]{2,1,0:T(8,128)(2,1)} %param.10), kind=kOutput, calls=%fused_computation.36 | convolution fusion | flops 38660997120 | bytes 72351744 | tf_op jit(solution)/shard_map/eskf,edf->eskd/dot_general | solution.py:58
  962.7 10.9 copy.24
  973.6 6.8 all-to-all-start.3
  981.1 177.1 %psum.23 = f32[768,8]{0,1:T(8,128)} all-reduce(f32[768,8]{0,1:T(8,128)S(1)} %convolution_bitcast_fusion), channel_id=1, replica_groups=mesh['dp'=8,'ep'=4] {'dp','ep'}, use_global_device_ids=true, to_apply=%region_10.11 | all-reduce | flops 6144 | bytes 49152 | tf_op jit(solution)/shard_map/psum | solution.py:67
  1158.2 16.7 gather_fusion.4
  1174.9 4.6 add_convert_fusion
  1179.5 859.7 %all-reduce.3.cloned.1.call-done = (f32[2,768,3072]{2,1,0:T(8,128)}, f32[2,3072,768]{2,1,0:T(8,128)}) async-done(((f32[2,768,3072]{2,1,0:T(8,128)}, f32[2,3072,768]{2,1,0:T(8,128)}), (f32[2,768,3072]{2,1,0:T(8,128)}, f32[2,3072,768]{2,1,0:T(8,128)})) %all-reduce.3.cloned.1.call-update) | async-done | bytes 37748752 | tf_op jit(solution)/shard_map/psum | solution.py:65
  2039.1 14.9 copy.54
  2054.0 1.8 slice-done.2
  2055.8 1.2 slice-done.3
  2057.6 6.8 copy.55
  (78 shorter events, 5.1 us)
Async XLA Ops:
  7.2 52.8 %copy-start = (bf16[2048,768]{1,0:T(8,128)(2,1)S(1)}, bf16[2048,768]{1,0:T(8,128)(2,1)}, u32[]{:S(2)}) copy-start(bf16[2048,768]{1,0:T(8,128)(2,1)} %param.6) | copy-start | bytes 9437188
  8.4 5.7 copy-start.21
  14.2 45.6 %copy-start.1 = (s32[2048]{0:T(1024)}, s32[2048]{0:T(1024)S(1)}, u32[]{:S(2)}) copy-start(s32[2048]{0:T(1024)S(1)} %get-tuple-element.7) | copy-start | bytes 24580
  59.9 34.6 %copy-start.7 = (s32[8192]{0:T(1024)}, s32[8192]{0:T(1024)S(1)}, u32[]{:S(2)}) copy-start(s32[8192]{0:T(1024)S(1)} %bitcast_clamp_fusion) | copy-start | bytes 98308
  60.0 34.5 %copy-start.11 = (pred[4,2,1024]{2,1,0:T(4,128)(4,1)}, pred[4,2,1024]{2,1,0:T(4,128)(4,1)S(1)}, u32[]{:S(2)}) copy-start(pred[4,2,1024]{2,1,0:T(4,128)(4,1)S(1)} %iota_compare_fusion.1) | copy-start | bytes 24580
  365.6 7.1 copy-start.2
  365.6 12.2 copy-start.22
  365.6 12.8 copy-start.19
  365.6 14.3 copy-start.5
  365.6 144.5 %all-to-all-start.1 = ((bf16[2,4,1024,768]{3,2,0,1:T(8,128)(2,1)}), bf16[2,4,1024,768]{3,2,0,1:T(8,128)(2,1)}, u32[]{:S(2)}, u32[]{:S(2)}) async-start(bf16[2,4,1024,768]{3,2,0,1:T(8,128)(2,1)} %copy.22), calls=%async_computation.1 | async-start | bytes 25165824 | tf_op jit(solution)/shard_map/all_to_all | solution.py:37
  372.1 1667.0 %all-reduce.3.cloned.1.call-start = ((), (), s32[]{:S(2)}) async-start(), calls=%async_computation.4 | async-start | bytes 75497472 | tf_op jit(solution)/shard_map/psum | solution.py:65
  379.4 0.6 copy-start.3
  379.4 0.7 copy-start.9
  380.0 0.6 copy-start.13
  380.0 0.6 copy-start.15
  385.4 124.7 %copy-start.17 = (s32[2048]{0:T(1024)}, s32[2048]{0:T(1024)S(1)}, u32[]{:S(2)}) copy-start(s32[2048]{0:T(1024)S(1)} %fusion.39) | copy-start | bytes 24580
  526.4 6.0 copy-start.8
  532.5 39.4 %copy-start.12 = (pred[4,2,1024]{2,1,0:T(4,128)(4,1)S(1)}, pred[4,2,1024]{2,1,0:T(4,128)(4,1)}, u32[]{:S(2)}) copy-start(pred[4,2,1024]{2,1,0:T(4,128)(4,1)} %copy-done.11) | copy-start | bytes 24580
  973.6 6.9 copy-start.16
  973.6 6.9 copy-start.23
  973.6 6.9 copy-start.4
  973.6 6.9 copy-start.6
  973.6 6.9 copy-start.10
  973.6 6.9 copy-start.14
  973.6 184.6 %copy-start.18 = (s32[2048]{0:T(1024)S(1)}, s32[2048]{0:T(1024)}, u32[]{:S(2)}) copy-start(s32[2048]{0:T(1024)} %copy-done.17) | copy-start | bytes 24580
  973.6 184.6 %all-to-all-start.3 = ((bf16[2,4,1024,768]{3,2,0,1:T(8,128)(2,1)}), bf16[2,4,1024,768]{3,2,0,1:T(8,128)(2,1)}, u32[]{:S(2)}, u32[]{:S(2)}) async-start(bf16[2,4,1024,768]{3,2,0,1:T(8,128)(2,1)} %copy.24), calls=%async_computation.3 | async-start | bytes 25165824 | tf_op jit(solution)/shard_map/all_to_all | solution.py:37
  1158.2 16.7 copy-start.20
  2039.1 14.9 slice-start
  2039.1 14.9 slice-start.1
  2039.1 16.6 slice-start.2
  2039.1 17.8 slice-start.3
  2039.1 18.4 slice-start.4
Sparse Core Ops, SparseCore 0:
  915.5 1123.5 all-reduce.2
where the time goes:
time: 2070 us
  waiting for transfers between devices  984 us (48%)
  blocking collectives  462 us (22%)
  matrix products  364 us (18%)
  local copies, waits for them, and re-layouts  195 us (9%)
  other arithmetic  36.8 us (2%)
    psum x1, waiting for transfers between devices, local_step(): grad_up = lax.psum(grad_up, 'dp')  860 us
    all_to_all x2, blocking collectives, dispatch(): return lax.all_to_all(picked, 'ep', 0, 0, tiled=True)  285 us
    psum x1, blocking collectives, local_step(): grad_gate = lax.psum(grad_gate, ('dp', 'ep'))  177 us
    all_to_all x2, waiting for transfers between devices, combine(): returned = lax.all_to_all(expert_rows, 'ep', 1, 0, tiled=True)  125 us
    dot_general x1, matrix products, local_step(): jnp.einsum('sekd,efd->eskf', recv_grad, w_down, preferred_element_type=jn...  98.3 us
    gather x2, local copies, waits for them, and re-layouts, dispatch(): tok_rows[src_tok]  73.8 us
    dot_general x1, matrix products, local_step(): jnp.einsum('sekd,edf->eskf', recv_rows, w_up, preferred_element_type=jnp....  70.2 us
    dot_general x1, matrix products, local_step(): jnp.einsum('eskf,sekd->efd', hidden, recv_grad, preferred_element_type=jn...  48.4 us
  transfers between devices with their start and end apart: 3, of which 2 were waited for; matrix products, arithmetic and copies ran while one was open for 4% of the time, Pallas kernels for 0%

commit v1 on v0

v1 whole, which is shorter than its diff:
```python
import jax
import jax.numpy as jnp
from jax import lax
from jax.sharding import PartitionSpec as P

PAD_FACTOR = 4
ROW_SIXTEENTHS = (3, 6, 10, 13, 16)


def solution(mesh):
    ep_size = mesh.shape['ep']
    dp_size = mesh.shape['dp']
    tok_spec = P(('dp', 'ep'), None)
    idx_spec = P(('dp', 'ep'))
    rep_spec = P(None, None)
    exp_spec = P('ep', None, None)

    def swap(value, bit):
        return lax.ppermute(value, 'ep', [(i, i ^ bit) for i in range(ep_size)])

    def expert_pass(rows):
        def run(x_all, dy_all, src, used, w1, w2):
            total = src.shape[0]
            pick = src[:rows]
            xs = x_all[pick]
            ds = jnp.where(jnp.arange(rows, dtype=jnp.int32)[:, None] < used, dy_all[pick], jnp.zeros((), dy_all.dtype))
            pre_act = jnp.dot(xs, w1, preferred_element_type=jnp.float32)
            hid_full, gelu_back = jax.vjp(jax.nn.gelu, pre_act)
            hidden = hid_full.astype(jnp.bfloat16)
            d_hidden = jnp.einsum('kd,fd->kf', ds, w2, preferred_element_type=jnp.float32)
            d_pre = gelu_back(d_hidden)[0].astype(jnp.bfloat16)
            grad_down = jnp.einsum('kf,kd->fd', hidden, ds, preferred_element_type=jnp.float32).astype(jnp.bfloat16)
            grad_up = jnp.einsum('kd,kf->df', xs, d_pre, preferred_element_type=jnp.float32).astype(jnp.bfloat16)
            y_rows = jnp.dot(hidden, w2, preferred_element_type=jnp.float32).astype(jnp.bfloat16)
            d_rows = jnp.einsum('kf,df->kd', d_pre, w1, preferred_element_type=jnp.float32).astype(jnp.bfloat16)
            tail = ((0, total - rows), (0, 0))
            return jnp.pad(y_rows, tail), jnp.pad(d_rows, tail), grad_up, grad_down

        return run

    def scatter_dp(part, my_dp):
        rows, cols = part.shape
        pieces = part.reshape(dp_size, rows // dp_size, cols)
        half = dp_size // 2
        got = [lax.dynamic_index_in_dim(pieces, my_dp, 0, keepdims=False)]
        for hop in range(1, dp_size):
            far, flip = hop // 2, hop % 2
            pairs = [(i, (i // 2 + far) % half * 2 + (i % 2 + flip) % 2) for i in range(dp_size)]
            target = (my_dp // 2 + far) % half * 2 + (my_dp + flip) % 2
            piece = lax.dynamic_index_in_dim(pieces, target, 0, keepdims=False)
            got.append(lax.ppermute(piece, 'dp', pairs))
        return got

    def gather_dp(got):
        total = got[0].astype(jnp.float32)
        for piece in got[1:]:
            total = total + piece.astype(jnp.float32)
        return lax.all_gather(total.astype(jnp.bfloat16), 'dp', axis=0, tiled=True)

    def local_step(x_loc, gy_loc, idx_loc, w_gate, w_up, w_down):
        tok_count, _ = x_loc.shape
        n_experts = w_gate.shape[1]
        local_experts = w_up.shape[0]
        max_rows = ep_size * PAD_FACTOR * tok_count // n_experts
        sizes = [max_rows * part // 16 for part in ROW_SIXTEENTHS]
        me = lax.axis_index('ep')
        my_dp = lax.axis_index('dp')
        onehot = idx_loc[:, None] == jnp.arange(n_experts, dtype=jnp.int32)[None, :]

        router_logit = jnp.dot(x_loc, w_gate, preferred_element_type=jnp.float32)
        router_prob = jax.nn.softmax(router_logit, axis=-1)
        gate_val = n_experts * jnp.sum(jnp.where(onehot, router_prob, 0.0), axis=1)
        gy_full = gy_loc.astype(jnp.float32)

        def dispatch(tok_rows):
            far_rows = swap(tok_rows, 2)
            near_rows = swap(tok_rows, 1)
            return jnp.concatenate([tok_rows, near_rows, far_rows, swap(far_rows, 1)], axis=0)

        x_all = dispatch(x_loc)
        gy_all = dispatch(gy_loc)

        def by_distance(value):
            group = lax.all_gather(value, 'ep')
            return [lax.dynamic_index_in_dim(group, me ^ j, 0, keepdims=False) for j in range(ep_size)]

        idx_rel = by_distance(idx_loc)
        gate_all = jnp.concatenate(by_distance(gate_val))
        dy_all = (gate_all[:, None] * gy_all.astype(jnp.float32)).astype(jnp.bfloat16)
        slot_exp = jnp.concatenate(idx_rel) - me * local_experts
        mine = (slot_exp >= 0) & (slot_exp < local_experts)
        key = jnp.where(mine, slot_exp, local_experts)
        order = jnp.argsort(key, stable=True).astype(jnp.int32)
        place = jnp.argsort(order).astype(jnp.int32)
        used = jnp.sum(key[:, None] == jnp.arange(local_experts, dtype=jnp.int32)[None, :], axis=0, dtype=jnp.int32)
        begin = jnp.cumsum(used) - used
        shift = sum(jnp.where(key == l, l * max_rows - begin[l], 0) for l in range(local_experts))
        slot = jnp.where(mine, place + shift, 0)
        order, slot = lax.optimization_barrier((order, slot))

        y_parts, d_parts, ups, downs = [], [], [], []
        for l in range(local_experts):
            src = lax.dynamic_slice(order, (begin[l],), (max_rows,))
            which = sum((used[l] > size).astype(jnp.int32) for size in sizes[:-1])
            y_rows, d_rows, grad_up, grad_down = lax.switch(
                which, [expert_pass(size) for size in sizes], x_all, dy_all, src, used[l], w_up[l], w_down[l])
            if l > 0:
                (y_rows, d_rows, grad_up, grad_down), downs[-1], ups[-1] = lax.optimization_barrier(
                    ((y_rows, d_rows, grad_up, grad_down), downs[-1], ups[-1]))
            y_parts.append(y_rows)
            d_parts.append(d_rows)
            downs.append(scatter_dp(grad_down, my_dp))
            ups.append(scatter_dp(grad_up, my_dp))

        def place_rows(parts):
            table = jnp.concatenate(parts, axis=0)
            slots = slot.reshape(ep_size, tok_count)
            out_rows = table[jnp.concatenate([slots[3], slots[1]])]
            keep_rows = table[jnp.concatenate([slots[2], slots[0]])]
            near_far = swap(out_rows[:tok_count], 1)
            near_own = swap(out_rows[tok_count:], 1)
            far_mine = (idx_rel[2] // local_experts == me)[:, None]
            return jnp.where(far_mine, keep_rows[:tok_count], near_far), keep_rows[tok_count:], near_own

        def combine(far_out, keep_own, near_own):
            owner = (idx_loc // local_experts)[:, None]
            return jnp.where(owner == me, keep_own, jnp.where(owner == (me ^ 1), near_own, swap(far_out, 2)))

        y_sent = place_rows(y_parts)
        d_sent = place_rows(d_parts)
        y_sent, d_sent, downs[-1], ups[-1] = lax.optimization_barrier((y_sent, d_sent, downs[-1], ups[-1]))
        y_tok = combine(*y_sent).astype(jnp.float32)
        dx_expert = combine(*d_sent).astype(jnp.float32)
        moe_out = (gate_val[:, None] * y_tok).astype(jnp.bfloat16)
        d_gate = jnp.sum(gy_full * y_tok, axis=1)
        d_logit = ((d_gate * gate_val)[:, None] * (onehot.astype(jnp.float32) - router_prob)).astype(jnp.bfloat16)
        dx_router = jnp.einsum('te,de->td', d_logit, w_gate, preferred_element_type=jnp.float32)
        grad_x = (dx_expert + dx_router).astype(jnp.bfloat16)
        grad_gate = jnp.einsum('td,te->de', x_loc, d_logit, preferred_element_type=jnp.float32)
        grad_gate = lax.psum(grad_gate, ('dp', 'ep'))
        grad_down = jnp.stack([gather_dp(got) for got in downs]).astype(jnp.float32)
        grad_up = jnp.stack([gather_dp(got) for got in ups]).astype(jnp.float32)
        return moe_out, grad_x, grad_up, grad_down, grad_gate

    return jax.shard_map(local_step, mesh=mesh, in_specs=(tok_spec, tok_spec, idx_spec, rep_spec, exp_spec, exp_spec), out_specs=(tok_spec, tok_spec, exp_spec, exp_spec, rep_spec), check_vma=False)
```

time: 2070 us -> 1400 us (0.68)
  waiting for transfers between devices: 984 us -> 306 us
  blocking collectives: 462 us -> 234 us
  starting transfers between devices: 13.9 us -> 223 us
  matrix products: 364 us -> 197 us
  other arithmetic: 36.8 us -> 107 us
  loops' own time: 0 us -> 56.6 us
  local copies, waits for them, and re-layouts: 195 us -> 242 us
    psum x1 -> x0, waiting for transfers between devices: 860 us -> none  [local_step(): grad_up = lax.psum(grad_up, 'dp')]
    all_to_all x2 -> x0, blocking collectives: 285 us -> none  [dispatch(): return lax.all_to_all(picked, 'ep', 0, 0, tiled=True)]
    ppermute x0 -> x40, waiting for transfers between devices: none -> 267 us  [the longest x28 198 us: scatter_dp(): got.append(lax.ppermute(piece, 'dp', pairs))]
    ppermute x0 -> x40, starting transfers between devices: none -> 223 us  [the longest x28 211 us: scatter_dp(): got.append(lax.ppermute(piece, 'dp', pairs))]
    dot_general x6 -> x12, matrix products: 358 us -> 188 us  [the longest x2 46 us: run(): jnp.einsum('kd,fd->kf', ds, w2, preferred_element_type=jnp.float32)]
    all_gather x0 -> x2, blocking collectives: none -> 142 us  [by_distance(): group = lax.all_gather(value, 'ep')]
    all_to_all x2 -> x0, waiting for transfers between devices: 125 us -> none  [combine(): returned = lax.all_to_all(expert_rows, 'ep', 1, 0, tiled=True)]
    psum x1, blocking collectives: 177 us -> 92.3 us  [local_step(): grad_gate = lax.psum(grad_gate, ('dp', 'ep'))]
  transfers between devices with their start and end apart: 3 -> 44, of which waited for: 2 -> 11; matrix products, arithmetic and copies ran while one was open for 4% -> 30% of each run, Pallas kernels for 0% -> 0%
where the time goes in v1:
time: 1400 us; the launch traced here: 1390 us
  waiting for transfers between devices  306 us (22%)
  local copies, waits for them, and re-layouts  242 us (17%)
  blocking collectives  234 us (17%)
  starting transfers between devices  223 us (16%)
  matrix products  197 us (14%)
  other arithmetic  107 us (8%)
  loops' own time  56.6 us (4%)
  between operations  23.1 us (2%)
    ppermute x28, starting transfers between devices, scatter_dp(): got.append(lax.ppermute(piece, 'dp', pairs))  211 us
    ppermute x28, waiting for transfers between devices, scatter_dp(): got.append(lax.ppermute(piece, 'dp', pairs))  198 us
    all_gather x2, blocking collectives, by_distance(): group = lax.all_gather(value, 'ep')  142 us
    psum x1, blocking collectives, local_step(): grad_gate = lax.psum(grad_gate, ('dp', 'ep'))  92.3 us
    ppermute x12, waiting for transfers between devices, swap(): return lax.ppermute(value, 'ep', [(i, i ^ bit) for i in range(ep_size)])  69.2 us
    gather x2, local copies, waits for them, and re-layouts, place_rows(): out_rows = table[jnp.concatenate([slots[3], slots[1]])]  50.8 us
    gather x2, local copies, waits for them, and re-layouts, place_rows(): keep_rows = table[jnp.concatenate([slots[2], slots[0]])]  50.6 us
    dot_general x2, matrix products, run(): jnp.einsum('kd,fd->kf', ds, w2, preferred_element_type=jnp.float32)  46 us
  transfers between devices with their start and end apart: 44, of which 11 were waited for; matrix products, arithmetic and copies ran while one was open for 30% of the time, Pallas kernels for 0%

profile of v1, /device:TPU:0, one launch (start us, length us, event | category | flops | bytes accessed | tf_op | source)
XLA Modules:
  0.0 1389.0 jit_solution(7087759096269180760)
XLA Ops:
  10.9 136.2 %all-gather = s32[8192]{0:T(1024)S(1)} all-gather(s32[2048]{0:T(1024)} %param.18), channel_id=2, replica_groups=mesh['dp'=8,'ep'=4] {'ep'}, dimensions={0}, use_global_device_ids=true | all-gather | bytes 40960 | tf_op jit(solution)/shard_map/all_gather | solution.py:84
  198.6 31.2 %multiply_convert_fusion.20 = bf16[8192,768]{1,0:T(8,128)(2,1)} fusion(bf16[2048,768]{1,0:T(8,128)(2,1)} %collective-permute-done.5, bf16[2048,768]{1,0:T(8,128)(2,1)S(1)} %collective-permute-done.4, bf16[2048,768]{1,0:T(8,128)(2,1)} %collective-permute-done.3, bf16[2048,768]{1,0:T(8,128)(2,1)S(1)} %copy-done.2, f32[8192]{0:T(1024)S(1)} %pad_maximum_fusion), kind=kLoop, calls=%fused_computation.271 | loop fusion | flops 62914560 | bytes 25198592 | tf_op jit(solution)/shard_map/convert_element_type | solution.py:89
  229.8 108.5 %conditional.3 = (bf16[4096,768]{1,0:T(8,128)(2,1)}, bf16[4096,768]{1,0:T(8,128)(2,1)}, bf16[8,96,3072]{2,1,0:T(8,128)(2,1)}, bf16[8,384,768]{2,1,0:T(8,128)(2,1)}) conditional(s32[]{:T(128)} %clamp.6, (s32[]{:T(128)}, s32[8192]{0:T(1024)S(1)}, bf16[8192,768]{1,0:T(8,128)(2,1)}, bf16[2,768,3072]{2,1,0:T(8,128)(2,1)}, ...), branch_computations={%region_7.8_spmd, %region_8.9_spmd, %region_9.10_spmd, %region_10.... | conditional | flops 116346339328 | bytes 390148320 | solution.py:105
  269.6 11.4 fusion.6
  347.2 78.8 %collective-permute-start.10 = (bf16[384,768]{1,0:T(8,128)(2,1)S(1)}, bf16[384,768]{1,0:T(8,128)(2,1)S(1)}, u32[]{:S(2)}, u32[]{:S(2)}) collective-permute-start(bf16[384,768]{1,0:T(8,128)(2,1)S(1)} %get-tuple-element.422), channel_id=1, source_target_pairs={{0,20},{4,16},{8,28},{12,24},{16,4},{20,0},{24,12},{28,8},{1,21},{... | collective-permute-start | bytes 1769480 | tf_op jit(solution)/shard_map/ppermute | solution.py:51
  435.4 57.4 %collective-permute-start.6 = (bf16[384,768]{1,0:T(8,128)(2,1)S(1)}, bf16[384,768]{1,0:T(8,128)(2,1)S(1)}, u32[]{:S(2)}, u32[]{:S(2)}) collective-permute-start(bf16[384,768]{1,0:T(8,128)(2,1)S(1)} %get-tuple-element.426), channel_id=1, source_target_pairs={{0,4},{4,0},{8,12},{12,8},{16,20},{20,16},{24,28},{28,24},{1,5},{5... | collective-permute-start | bytes 1769480 | tf_op jit(solution)/shard_map/ppermute | solution.py:51
  493.4 35.3 %collective-permute-done.9 = bf16[384,768]{1,0:T(8,128)(2,1)S(1)} collective-permute-done((bf16[384,768]{1,0:T(8,128)(2,1)S(1)}, bf16[384,768]{1,0:T(8,128)(2,1)S(1)}, u32[]{:S(2)}, u32[]{:S(2)}) %collective-permute-start.9) | collective-permute-done | bytes 589856 | tf_op jit(solution)/shard_map/ppermute | solution.py:51
  539.2 13.0 collective-permute-done.18
  552.2 41.7 %collective-permute-start.13 = (bf16[96,3072]{1,0:T(8,128)(2,1)}, bf16[96,3072]{1,0:T(8,128)(2,1)}, u32[]{:S(2)}, u32[]{:S(2)}) collective-permute-start(bf16[96,3072]{1,0:T(8,128)(2,1)} %get-tuple-element.418), channel_id=1, source_target_pairs={{0,4},{4,0},{8,12},{12,8},{16,20},{20,16},{24,28},{28,24},{1,5},{5... | collective-permute-start | bytes 1769480 | tf_op jit(solution)/shard_map/ppermute | solution.py:51
  596.4 201.3 %conditional.4 = (bf16[4096,768]{1,0:T(8,128)(2,1)}, bf16[4096,768]{1,0:T(8,128)(2,1)}, bf16[768,3072]{1,0:T(8,128)(2,1)}, bf16[3072,768]{1,0:T(8,128)(2,1)}) conditional(s32[]{:T(128)} %clamp.7, (s32[4096]{0:T(1024)S(1)}, bf16[8192,768]{1,0:T(8,128)(2,1)}, bf16[768,3072]{1,0:T(8,128)(2,1)}, ...), branch_computations={%region_12.13_spmd, %region_13.14_spmd, %region_14.15_spmd, %regio... | conditional | flops 116341620736 | bytes 401158336
  604.7 16.5 %gather_fusion.11 = bf16[2560,768]{1,0:T(8,128)(2,1)} fusion(bf16[8192,768]{1,0:T(8,128)(2,1)} %get-tuple-element.250, s32[3072]{0:T(1024)S(1)} %pad_clamp_fusion.6), kind=kCustom, calls=%fused_computation.15 | custom fusion | bytes 7874560 | tf_op jit(solution)/shard_map/cond/branch_2_fun/gather | solution.py:26
  621.2 16.5 %gather_fusion.10 = bf16[2560,768]{1,0:T(8,128)(2,1)} fusion(bf16[8192,768]{1,0:T(8,128)(2,1)} %get-tuple-element.245, s32[3072]{0:T(1024)S(1)} %pad_clamp_fusion.6), kind=kCustom, calls=%fused_computation.14 | custom fusion | bytes 7874560 | tf_op jit(solution)/shard_map/cond/branch_2_fun/gather | solution.py:25
  637.8 21.1 %fusion.190 = f32[2560,3072]{1,0:T(8,128)} fusion(bf16[2560,768]{1,0:T(8,128)(2,1)} %gather_fusion.10, bf16[768,3072]{1,0:T(8,128)(2,1)} %get-tuple-element.247), kind=kOutput, calls=%fused_computation.387 | convolution fusion | flops 12079595520 | bytes 40108032 | tf_op jit(solution)/shard_map/cond/branch_2_fun/dot_general | solution.py:27
  658.9 23.1 %convolution_convert_fusion.21 = bf16[2560,768]{1,0:T(8,128)(2,1)S(1)} fusion(bf16[3072,768]{1,0:T(8,128)(2,1)S(1)} %bitcast.285, f32[2560,3072]{1,0:T(8,128)} %fusion.190), kind=kOutput, calls=%fused_computation.225 | convolution fusion | flops 12152340480 | bytes 40108032 | tf_op jit(solution)/shard_map/cond/branch_2_fun/dot_general | solution.py:34
  685.0 26.6 %fusion.141 = bf16[3072,768]{1,0:T(8,128)(2,1)} fusion(bf16[2560,768]{1,0:T(8,128)(2,1)} %gather_fusion.11, pred[2560]{0:T(1024)(128)(4,1)S(1)} %iota_compare_fusion.7, f32[2560,3072]{1,0:T(8,128)} %fusion.190), kind=kOutput, calls=%fused_computation.227 | convolution fusion | flops 12152340480 | bytes 40110592 | tf_op jit(solution)/shard_map/cond/branch_2_fun/kf,kd->fd/dot_general | solution.py:32
  711.5 34.6 %fusion.140 = bf16[2560,3072]{1,0:T(8,128)(2,1)} fusion(f32[2560,3072]{1,0:T(8,128)} %fusion.190, bf16[3072,768]{1,0:T(8,128)(2,1)} %get-tuple-element.248, bf16[2560,768]{1,0:T(8,128)(2,1)} %gather_fusion.11, pred[2560]{0:T(1024)(128)(4,1)S(1)} %iota_compare_fusion.7), kind=kOutput, calls=%fused_computation.222 | convolution fusion | flops 12238848000 | bytes 55839232 | tf_op jit(solution)/shard_map/cond/branch_2_fun/kd,fd->kf/dot_general | solution.py:30
  746.1 15.6 %convolution_convert_fusion.20 = bf16[2560,768]{1,0:T(8,128)(2,1)S(1)} fusion(bf16[2560,3072]{1,0:T(8,128)(2,1)} %fusion.140, bf16[768,3072]{1,0:T(8,128)(2,1)S(1)} %bitcast.275), kind=kOutput, calls=%fused_computation.224 | convolution fusion | flops 12081561600 | bytes 24379392 | tf_op jit(solution)/shard_map/cond/branch_2_fun/kf,df->kd/dot_general | solution.py:35
  761.8 18.2 %fusion.191 = bf16[768,3072]{1,0:T(8,128)(2,1)} fusion(bf16[2560,768]{1,0:T(8,128)(2,1)S(1)} %copy-done.7, bf16[2560,3072]{1,0:T(8,128)(2,1)} %fusion.140), kind=kOutput, calls=%fused_computation.388 | convolution fusion | flops 12079595520 | bytes 24379392 | tf_op jit(solution)/shard_map/cond/branch_2_fun/kd,kf->df/dot_general | solution.py:33
  827.7 25.4 %gather_fusion.23 = bf16[4096,768]{1,0:T(8,128)(2,1)} fusion(bf16[8192,768]{1,0:T(8,128)(2,1)} %constant_dynamic-update-slice_fusion.6, s32[4096]{0:T(1024)S(1)} %broadcast_clamp_fusion), kind=kCustom, calls=%fused_computation.23 | custom fusion | bytes 12599296 | tf_op jit(solution)/shard_map/gather | solution.py:118
  869.1 25.4 %gather_fusion.21 = bf16[4096,768]{1,0:T(8,128)(2,1)} fusion(bf16[8192,768]{1,0:T(8,128)(2,1)} %constant_dynamic-update-slice_fusion.4, s32[4096]{0:T(1024)S(1)} %broadcast_clamp_fusion), kind=kCustom, calls=%fused_computation.21 | custom fusion | bytes 12599296 | tf_op jit(solution)/shard_map/gather | solution.py:118
  905.3 57.4 %collective-permute-done.27 = bf16[384,768]{1,0:T(8,128)(2,1)S(1)} collective-permute-done((bf16[384,768]{1,0:T(8,128)(2,1)S(1)}, bf16[384,768]{1,0:T(8,128)(2,1)S(1)}, u32[]{:S(2)}, u32[]{:S(2)}) %collective-permute-start.27) | collective-permute-done | bytes 589856 | tf_op jit(solution)/shard_map/ppermute | solution.py:51
  978.0 15.4 %collective-permute-done.37 = bf16[96,3072]{1,0:T(8,128)(2,1)S(1)} collective-permute-done((bf16[96,3072]{1,0:T(8,128)(2,1)S(1)}, bf16[96,3072]{1,0:T(8,128)(2,1)S(1)}, u32[]{:S(2)}, u32[]{:S(2)}) %collective-permute-start.37) | collective-permute-done | bytes 589856 | tf_op jit(solution)/shard_map/ppermute | solution.py:51
  994.9 25.3 %gather_fusion.22 = bf16[4096,768]{1,0:T(8,128)(2,1)} fusion(bf16[8192,768]{1,0:T(8,128)(2,1)} %constant_dynamic-update-slice_fusion.6, s32[4096]{0:T(1024)S(1)} %broadcast_clamp_fusion.1), kind=kCustom, calls=%fused_computation.22 | custom fusion | bytes 12599296 | tf_op jit(solution)/shard_map/gather | solution.py:119
  1020.2 25.2 %gather_fusion.20 = bf16[4096,768]{1,0:T(8,128)(2,1)} fusion(bf16[8192,768]{1,0:T(8,128)(2,1)} %constant_dynamic-update-slice_fusion.4, s32[4096]{0:T(1024)S(1)} %broadcast_clamp_fusion.1), kind=kCustom, calls=%fused_computation.20 | custom fusion | bytes 12599296 | tf_op jit(solution)/shard_map/gather | solution.py:119
  1055.2 31.2 %collective-permute-done.35 = bf16[96,3072]{1,0:T(8,128)(2,1)S(1)} collective-permute-done((bf16[96,3072]{1,0:T(8,128)(2,1)}, bf16[96,3072]{1,0:T(8,128)(2,1)S(1)}, u32[]{:S(2)}, u32[]{:S(2)}) %collective-permute-start.35) | collective-permute-done | bytes 589856 | tf_op jit(solution)/shard_map/ppermute | solution.py:51
  1086.5 24.3 %collective-permute-done.34 = bf16[96,3072]{1,0:T(8,128)(2,1)S(1)} collective-permute-done((bf16[96,3072]{1,0:T(8,128)(2,1)}, bf16[96,3072]{1,0:T(8,128)(2,1)S(1)}, u32[]{:S(2)}, u32[]{:S(2)}) %collective-permute-start.34) | collective-permute-done | bytes 589856 | tf_op jit(solution)/shard_map/ppermute | solution.py:51
  1116.9 11.0 collective-permute-done.32
  1141.4 69.1 %collective-permute-done.38 = bf16[2048,768]{1,0:T(8,128)(2,1)S(1)} collective-permute-done((bf16[2048,768]{1,0:T(8,128)(2,1)}, bf16[2048,768]{1,0:T(8,128)(2,1)S(1)}, u32[]{:S(2)}, u32[]{:S(2)}) %collective-permute-start.38) | collective-permute-done | bytes 3145760 | tf_op jit(solution)/shard_map/ppermute | solution.py:19
  1217.3 92.3 %psum.7 = f32[768,8]{0,1:T(8,128)} all-reduce(f32[768,8]{0,1:T(8,128)S(1)} %convolution_bitcast_fusion), channel_id=1, replica_groups=mesh['dp'=8,'ep'=4] {'dp','ep'}, use_global_device_ids=true, to_apply=%region_18.19 | all-reduce | flops 6144 | bytes 49152 | tf_op jit(solution)/shard_map/psum | solution.py:140
  1319.6 11.8 maximum_convert_fusion.1
  1331.5 39.0 %all-gather.9.cloned.1.call-done = bf16[768,3072]{1,0:T(8,128)(2,1)} async-done(((bf16[96,3072]{1,0:T(8,128)(2,1)}), bf16[768,3072]{1,0:T(8,128)(2,1)}) %all-gather.9.cloned.1.call-update) | async-done | bytes 4718608 | tf_op jit(solution)/shard_map/all_gather | solution.py:58
  1370.4 11.8 maximum_convert_fusion
  (308 shorter events, 267.4 us)
Async XLA Ops:
  7.2 1312.4 %all-gather.11.cloned.1.call-start = ((), (), s32[]{:S(2)}) async-start(), calls=%async_computation.2 | async-start | bytes 5308416 | tf_op jit(solution)/shard_map/all_gather | solution.py:58
  7.2 139.8 %collective-permute-start.1 = (bf16[2048,768]{1,0:T(8,128)(2,1)}, bf16[2048,768]{1,0:T(8,128)(2,1)}, u32[]{:S(2)}, u32[]{:S(2)}) collective-permute-start(bf16[2048,768]{1,0:T(8,128)(2,1)} %param.16), channel_id=1, source_target_pairs={{0,2},{1,3},{2,0},{3,1},{4,6},{5,7},{6,4},{7,5},{8,10},{9,11},{10,... | collective-permute-start | bytes 9437192 | tf_op jit(solution)/shard_map/ppermute | solution.py:19
  10.3 137.3 %collective-permute-start.4 = (bf16[2048,768]{1,0:T(8,128)(2,1)}, bf16[2048,768]{1,0:T(8,128)(2,1)S(1)}, u32[]{:S(2)}, u32[]{:S(2)}) collective-permute-start(bf16[2048,768]{1,0:T(8,128)(2,1)} %param.17), channel_id=1, source_target_pairs={{0,2},{1,3},{2,0},{3,1},{4,6},{5,7},{6,4},{7,5},{8,10},{9,11},{10,... | collective-permute-start | bytes 9437192 | tf_op jit(solution)/shard_map/ppermute | solution.py:19
  10.3 176.8 %collective-permute-start = (bf16[2048,768]{1,0:T(8,128)(2,1)}, bf16[2048,768]{1,0:T(8,128)(2,1)}, u32[]{:S(2)}, u32[]{:S(2)}) collective-permute-start(bf16[2048,768]{1,0:T(8,128)(2,1)} %param.16), channel_id=1, source_target_pairs={{0,1},{1,0},{2,3},{3,2},{4,5},{5,4},{6,7},{7,6},{8,9},{9,8},{10,11... | collective-permute-start | bytes 9437192 | tf_op jit(solution)/shard_map/ppermute | solution.py:19
  10.3 188.2 %collective-permute-start.3 = (bf16[2048,768]{1,0:T(8,128)(2,1)}, bf16[2048,768]{1,0:T(8,128)(2,1)}, u32[]{:S(2)}, u32[]{:S(2)}) collective-permute-start(bf16[2048,768]{1,0:T(8,128)(2,1)} %param.17), channel_id=1, source_target_pairs={{0,1},{1,0},{2,3},{3,2},{4,5},{5,4},{6,7},{7,6},{8,9},{9,8},{10,11... | collective-permute-start | bytes 9437192 | tf_op jit(solution)/shard_map/ppermute | solution.py:19
  342.0 91.9 %collective-permute-start.12 = (bf16[384,768]{1,0:T(8,128)(2,1)S(1)}, bf16[384,768]{1,0:T(8,128)(2,1)S(1)}, u32[]{:S(2)}, u32[]{:S(2)}) collective-permute-start(bf16[384,768]{1,0:T(8,128)(2,1)S(1)} %get-tuple-element.420), channel_id=1, source_target_pairs={{0,28},{4,24},{8,4},{12,0},{16,12},{20,8},{24,20},{28,16},{1,29},{... | collective-permute-start | bytes 1769480 | tf_op jit(solution)/shard_map/ppermute | solution.py:51
  342.0 93.4 %collective-permute-start.11 = (bf16[384,768]{1,0:T(8,128)(2,1)S(1)}, bf16[384,768]{1,0:T(8,128)(2,1)S(1)}, u32[]{:S(2)}, u32[]{:S(2)}) collective-permute-start(bf16[384,768]{1,0:T(8,128)(2,1)S(1)} %get-tuple-element.421), channel_id=1, source_target_pairs={{0,24},{4,28},{8,0},{12,4},{16,8},{20,12},{24,16},{28,20},{1,25},{... | collective-permute-start | bytes 1769480 | tf_op jit(solution)/shard_map/ppermute | solution.py:51
  347.2 146.2 %collective-permute-start.10 = (bf16[384,768]{1,0:T(8,128)(2,1)S(1)}, bf16[384,768]{1,0:T(8,128)(2,1)S(1)}, u32[]{:S(2)}, u32[]{:S(2)}) collective-permute-start(bf16[384,768]{1,0:T(8,128)(2,1)S(1)} %get-tuple-element.422), channel_id=1, source_target_pairs={{0,20},{4,16},{8,28},{12,24},{16,4},{20,0},{24,12},{28,8},{1,21},{... | collective-permute-start | bytes 1769480 | tf_op jit(solution)/shard_map/ppermute | solution.py:51
  426.0 102.7 %collective-permute-start.9 = (bf16[384,768]{1,0:T(8,128)(2,1)S(1)}, bf16[384,768]{1,0:T(8,128)(2,1)S(1)}, u32[]{:S(2)}, u32[]{:S(2)}) collective-permute-start(bf16[384,768]{1,0:T(8,128)(2,1)S(1)} %get-tuple-element.423), channel_id=1, source_target_pairs={{0,16},{4,20},{8,24},{12,28},{16,0},{20,4},{24,8},{28,12},{1,17},{... | collective-permute-start | bytes 1769480 | tf_op jit(solution)/shard_map/ppermute | solution.py:51
  426.6 105.4 %collective-permute-start.8 = (bf16[384,768]{1,0:T(8,128)(2,1)S(1)}, bf16[384,768]{1,0:T(8,128)(2,1)S(1)}, u32[]{:S(2)}, u32[]{:S(2)}) collective-permute-start(bf16[384,768]{1,0:T(8,128)(2,1)S(1)} %get-tuple-element.424), channel_id=1, source_target_pairs={{0,12},{4,8},{8,20},{12,16},{16,28},{20,24},{24,4},{28,0},{1,13},{... | collective-permute-start | bytes 1769480 | tf_op jit(solution)/shard_map/ppermute | solution.py:51
  433.9 98.2 %collective-permute-start.7 = (bf16[384,768]{1,0:T(8,128)(2,1)S(1)}, bf16[384,768]{1,0:T(8,128)(2,1)S(1)}, u32[]{:S(2)}, u32[]{:S(2)}) collective-permute-start(bf16[384,768]{1,0:T(8,128)(2,1)S(1)} %get-tuple-element.425), channel_id=1, source_target_pairs={{0,8},{4,12},{8,16},{12,20},{16,24},{20,28},{24,0},{28,4},{1,9},{5... | collective-permute-start | bytes 1769480 | tf_op jit(solution)/shard_map/ppermute | solution.py:51
  435.4 96.8 %collective-permute-start.6 = (bf16[384,768]{1,0:T(8,128)(2,1)S(1)}, bf16[384,768]{1,0:T(8,128)(2,1)S(1)}, u32[]{:S(2)}, u32[]{:S(2)}) collective-permute-start(bf16[384,768]{1,0:T(8,128)(2,1)S(1)} %get-tuple-element.426), channel_id=1, source_target_pairs={{0,4},{4,0},{8,12},{12,8},{16,20},{20,16},{24,28},{28,24},{1,5},{5... | collective-permute-start | bytes 1769480 | tf_op jit(solution)/shard_map/ppermute | solution.py:51
  532.1 265.7 %collective-permute-start.17 = (bf16[96,3072]{1,0:T(8,128)(2,1)}, bf16[96,3072]{1,0:T(8,128)(2,1)}, u32[]{:S(2)}, u32[]{:S(2)}) collective-permute-start(bf16[96,3072]{1,0:T(8,128)(2,1)} %get-tuple-element.414), channel_id=1, source_target_pairs={{0,20},{4,16},{8,28},{12,24},{16,4},{20,0},{24,12},{28,8},{1,21},{... | collective-permute-start | bytes 1769480 | tf_op jit(solution)/shard_map/ppermute | solution.py:51
  532.1 265.7 %collective-permute-start.16 = (bf16[96,3072]{1,0:T(8,128)(2,1)}, bf16[96,3072]{1,0:T(8,128)(2,1)}, u32[]{:S(2)}, u32[]{:S(2)}) collective-permute-start(bf16[96,3072]{1,0:T(8,128)(2,1)} %get-tuple-element.415), channel_id=1, source_target_pairs={{0,16},{4,20},{8,24},{12,28},{16,0},{20,4},{24,8},{28,12},{1,17},{... | collective-permute-start | bytes 1769480 | tf_op jit(solution)/shard_map/ppermute | solution.py:51
  532.2 265.6 %collective-permute-start.15 = (bf16[96,3072]{1,0:T(8,128)(2,1)}, bf16[96,3072]{1,0:T(8,128)(2,1)}, u32[]{:S(2)}, u32[]{:S(2)}) collective-permute-start(bf16[96,3072]{1,0:T(8,128)(2,1)} %get-tuple-element.416), channel_id=1, source_target_pairs={{0,12},{4,8},{8,20},{12,16},{16,28},{20,24},{24,4},{28,0},{1,13},{... | collective-permute-start | bytes 1769480 | tf_op jit(solution)/shard_map/ppermute | solution.py:51
  537.9 259.9 %collective-permute-start.14 = (bf16[96,3072]{1,0:T(8,128)(2,1)}, bf16[96,3072]{1,0:T(8,128)(2,1)}, u32[]{:S(2)}, u32[]{:S(2)}) collective-permute-start(bf16[96,3072]{1,0:T(8,128)(2,1)} %get-tuple-element.417), channel_id=1, source_target_pairs={{0,8},{4,12},{8,16},{12,20},{16,24},{20,28},{24,0},{28,4},{1,9},{5... | collective-permute-start | bytes 1769480 | tf_op jit(solution)/shard_map/ppermute | solution.py:51
  552.2 245.6 %collective-permute-start.13 = (bf16[96,3072]{1,0:T(8,128)(2,1)}, bf16[96,3072]{1,0:T(8,128)(2,1)}, u32[]{:S(2)}, u32[]{:S(2)}) collective-permute-start(bf16[96,3072]{1,0:T(8,128)(2,1)} %get-tuple-element.418), channel_id=1, source_target_pairs={{0,4},{4,0},{8,12},{12,8},{16,20},{20,16},{24,28},{28,24},{1,5},{5... | collective-permute-start | bytes 1769480 | tf_op jit(solution)/shard_map/ppermute | solution.py:51
  801.5 518.1 %all-gather.13.cloned.1.call-start = ((), (), s32[]{:S(2)}) async-start(), calls=%async_computation.3 | async-start | bytes 5308416 | tf_op jit(solution)/shard_map/all_gather | solution.py:58
  817.4 83.4 %collective-permute-start.30 = (bf16[384,768]{1,0:T(8,128)(2,1)}, bf16[384,768]{1,0:T(8,128)(2,1)}, u32[]{:S(2)}, u32[]{:S(2)}) collective-permute-start(bf16[384,768]{1,0:T(8,128)(2,1)} %get-tuple-element.404), channel_id=1, source_target_pairs={{0,28},{4,24},{8,4},{12,0},{16,12},{20,8},{24,20},{28,16},{1,29},{... | collective-permute-start | bytes 1769480 | tf_op jit(solution)/shard_map/ppermute | solution.py:51
  817.4 84.0 %collective-permute-start.29 = (bf16[384,768]{1,0:T(8,128)(2,1)}, bf16[384,768]{1,0:T(8,128)(2,1)}, u32[]{:S(2)}, u32[]{:S(2)}) collective-permute-start(bf16[384,768]{1,0:T(8,128)(2,1)} %get-tuple-element.405), channel_id=1, source_target_pairs={{0,24},{4,28},{8,0},{12,4},{16,8},{20,12},{24,16},{28,20},{1,25},{... | collective-permute-start | bytes 1769480 | tf_op jit(solution)/shard_map/ppermute | solution.py:51
  817.5 86.1 %collective-permute-start.28 = (bf16[384,768]{1,0:T(8,128)(2,1)}, bf16[384,768]{1,0:T(8,128)(2,1)}, u32[]{:S(2)}, u32[]{:S(2)}) collective-permute-start(bf16[384,768]{1,0:T(8,128)(2,1)} %get-tuple-element.406), channel_id=1, source_target_pairs={{0,20},{4,16},{8,28},{12,24},{16,4},{20,0},{24,12},{28,8},{1,21},{... | collective-permute-start | bytes 1769480 | tf_op jit(solution)/shard_map/ppermute | solution.py:51
  858.0 187.6 %collective-permute-start.22 = (bf16[2048,768]{1,0:T(8,128)(2,1)}, bf16[2048,768]{1,0:T(8,128)(2,1)}, u32[]{:S(2)}, u32[]{:S(2)}) collective-permute-start(bf16[2048,768]{1,0:T(8,128)(2,1)} %get-tuple-element.389), channel_id=1, source_target_pairs={{0,1},{1,0},{2,3},{3,2},{4,5},{5,4},{6,7},{7,6},{8,9},{9,8},{10,11... | collective-permute-start | bytes 9437192 | tf_op jit(solution)/shard_map/ppermute | solution.py:19
  900.6 210.2 %collective-permute-start.20 = (bf16[2048,768]{1,0:T(8,128)(2,1)}, bf16[2048,768]{1,0:T(8,128)(2,1)}, u32[]{:S(2)}, u32[]{:S(2)}) collective-permute-start(bf16[2048,768]{1,0:T(8,128)(2,1)} %get-tuple-element.393), channel_id=1, source_target_pairs={{0,1},{1,0},{2,3},{3,2},{4,5},{5,4},{6,7},{7,6},{8,9},{9,8},{10,11... | collective-permute-start | bytes 9437192 | tf_op jit(solution)/shard_map/ppermute | solution.py:19
  900.8 61.8 %collective-permute-start.27 = (bf16[384,768]{1,0:T(8,128)(2,1)S(1)}, bf16[384,768]{1,0:T(8,128)(2,1)S(1)}, u32[]{:S(2)}, u32[]{:S(2)}) collective-permute-start(bf16[384,768]{1,0:T(8,128)(2,1)S(1)} %copy-done.19), channel_id=1, source_target_pairs={{0,16},{4,20},{8,24},{12,28},{16,0},{20,4},{24,8},{28,12},{1,17},{... | collective-permute-start | bytes 1769480 | tf_op jit(solution)/shard_map/ppermute | solution.py:51
  901.4 61.8 %collective-permute-start.26 = (bf16[384,768]{1,0:T(8,128)(2,1)S(1)}, bf16[384,768]{1,0:T(8,128)(2,1)S(1)}, u32[]{:S(2)}, u32[]{:S(2)}) collective-permute-start(bf16[384,768]{1,0:T(8,128)(2,1)S(1)} %copy-done.18), channel_id=1, source_target_pairs={{0,12},{4,8},{8,20},{12,16},{16,28},{20,24},{24,4},{28,0},{1,13},{... | collective-permute-start | bytes 1769480 | tf_op jit(solution)/shard_map/ppermute | solution.py:51
  963.2 164.7 %collective-permute-start.23 = (bf16[2048,768]{1,0:T(8,128)(2,1)S(1)}, bf16[2048,768]{1,0:T(8,128)(2,1)}, u32[]{:S(2)}, u32[]{:S(2)}) collective-permute-start(bf16[2048,768]{1,0:T(8,128)(2,1)S(1)} %get-tuple-element.388), channel_id=1, source_target_pairs={{0,1},{1,0},{2,3},{3,2},{4,5},{5,4},{6,7},{7,6},{8,9},{9,8},{10,11... | collective-permute-start | bytes 9437192 | tf_op jit(solution)/shard_map/ppermute | solution.py:19
  963.3 164.6 %collective-permute-start.21 = (bf16[2048,768]{1,0:T(8,128)(2,1)}, bf16[2048,768]{1,0:T(8,128)(2,1)}, u32[]{:S(2)}, u32[]{:S(2)}) collective-permute-start(bf16[2048,768]{1,0:T(8,128)(2,1)} %get-tuple-element.392), channel_id=1, source_target_pairs={{0,1},{1,0},{2,3},{3,2},{4,5},{5,4},{6,7},{7,6},{8,9},{9,8},{10,11... | collective-permute-start | bytes 9437192 | tf_op jit(solution)/shard_map/ppermute | solution.py:19
  1045.6 65.3 %collective-permute-start.34 = (bf16[96,3072]{1,0:T(8,128)(2,1)}, bf16[96,3072]{1,0:T(8,128)(2,1)S(1)}, u32[]{:S(2)}, u32[]{:S(2)}) collective-permute-start(bf16[96,3072]{1,0:T(8,128)(2,1)} %get-tuple-element.399), channel_id=1, source_target_pairs={{0,16},{4,20},{8,24},{12,28},{16,0},{20,4},{24,8},{28,12},{1,17},{... | collective-permute-start | bytes 1769480 | tf_op jit(solution)/shard_map/ppermute | solution.py:51
  1132.0 199.5 %all-gather.7.cloned.1.call-start = ((), (), s32[]{:S(2)}) async-start(), calls=%async_computation | async-start | bytes 5308416 | tf_op jit(solution)/shard_map/all_gather | solution.py:58
  1136.0 234.4 %all-gather.9.cloned.1.call-start = ((), (), s32[]{:S(2)}) async-start(), calls=%async_computation.1 | async-start | bytes 5308416 | tf_op jit(solution)/shard_map/all_gather | solution.py:58
  1139.3 71.2 %collective-permute-start.38 = (bf16[2048,768]{1,0:T(8,128)(2,1)}, bf16[2048,768]{1,0:T(8,128)(2,1)S(1)}, u32[]{:S(2)}, u32[]{:S(2)}) collective-permute-start(bf16[2048,768]{1,0:T(8,128)(2,1)} %get-tuple-element.340), channel_id=1, source_target_pairs={{0,2},{1,3},{2,0},{3,1},{4,6},{5,7},{6,4},{7,5},{8,10},{9,11},{10,... | collective-permute-start | bytes 9437192 | tf_op jit(solution)/shard_map/ppermute | solution.py:19
  1139.4 174.4 %collective-permute-start.39 = (bf16[2048,768]{1,0:T(8,128)(2,1)}, bf16[2048,768]{1,0:T(8,128)(2,1)}, u32[]{:S(2)}, u32[]{:S(2)}) collective-permute-start(bf16[2048,768]{1,0:T(8,128)(2,1)} %get-tuple-element.343), channel_id=1, source_target_pairs={{0,2},{1,3},{2,0},{3,1},{4,6},{5,7},{6,4},{7,5},{8,10},{9,11},{10,... | collective-permute-start | bytes 9437192 | tf_op jit(solution)/shard_map/ppermute | solution.py:19
  (87 other events, 4454.8 us)
Sparse Core Ops, SparseCore 0:
  801.7 153.3 all-gather.10
  1132.1 77.4 all-gather.12
  1211.8 78.5 all-gather.6
  1292.9 77.4 all-gather.8

commit v2 on v1

--- a/solution.py
+++ b/solution.py
@@ -77,15 +77,15 @@
             near_rows = swap(tok_rows, 1)
             return jnp.concatenate([tok_rows, near_rows, far_rows, swap(far_rows, 1)], axis=0)
 
-        x_all = dispatch(x_loc)
-        gy_all = dispatch(gy_loc)
+        x_sent, gy_sent, idx_group = lax.optimization_barrier((x_loc, gy_loc, lax.all_gather(idx_loc, 'ep')))
+        x_all = dispatch(x_sent)
+        gy_all = dispatch(gy_sent)
 
-        def by_distance(value):
-            group = lax.all_gather(value, 'ep')
+        def by_distance(group):
             return [lax.dynamic_index_in_dim(group, me ^ j, 0, keepdims=False) for j in range(ep_size)]
 
-        idx_rel = by_distance(idx_loc)
-        gate_all = jnp.concatenate(by_distance(gate_val))
+        idx_rel = by_distance(idx_group)
+        gate_all = jnp.concatenate(by_distance(lax.all_gather(gate_val, 'ep')))
         dy_all = (gate_all[:, None] * gy_all.astype(jnp.float32)).astype(jnp.bfloat16)
         slot_exp = jnp.concatenate(idx_rel) - me * local_experts
         mine = (slot_exp >= 0) & (slot_exp < local_experts)

time: 1400 us -> 1400 us (level)
  waiting for transfers between devices: 306 us -> 442 us
  blocking collectives: 234 us -> 104 us
    ppermute x12, waiting for transfers between devices: 69.2 us -> 205 us  [swap(): return lax.ppermute(value, 'ep', [(i, i ^ bit) for i in range(ep_size)])]
    all_gather x2, blocking collectives: 142 us -> 12 us  [the longest x1 6.42 us: local_step(): lax.all_gather(idx_loc, 'ep')]
  transfers between devices with their start and end apart: 44 -> 44, of which waited for: 11 -> 13; matrix products, arithmetic and copies ran while one was open for 30% -> 30% of each run, Pallas kernels for 0% -> 0%
where the time goes in v2:
time: 1400 us; the launch traced here: 1390 us
  waiting for transfers between devices  442 us (32%)
  local copies, waits for them, and re-layouts  242 us (17%)
  starting transfers between devices  222 us (16%)
  matrix products  197 us (14%)
  other arithmetic  107 us (8%)
  blocking collectives  104 us (7%)
  loops' own time  56.6 us (4%)
  between operations  23.1 us (2%)
    ppermute x28, starting transfers between devices, scatter_dp(): got.append(lax.ppermute(piece, 'dp', pairs))  211 us
    ppermute x12, waiting for transfers between devices, swap(): return lax.ppermute(value, 'ep', [(i, i ^ bit) for i in range(ep_size)])  205 us
    ppermute x28, waiting for transfers between devices, scatter_dp(): got.append(lax.ppermute(piece, 'dp', pairs))  198 us
    psum x1, blocking collectives, local_step(): grad_gate = lax.psum(grad_gate, ('dp', 'ep'))  92.3 us
    gather x2, local copies, waits for them, and re-layouts, place_rows(): out_rows = table[jnp.concatenate([slots[3], slots[1]])]  50.8 us
    gather x2, local copies, waits for them, and re-layouts, place_rows(): keep_rows = table[jnp.concatenate([slots[2], slots[0]])]  50.6 us
    dot_general x2, matrix products, run(): jnp.einsum('kd,fd->kf', ds, w2, preferred_element_type=jnp.float32)  46 us
    all_gather x4, waiting for transfers between devices, gather_dp(): return lax.all_gather(total.astype(jnp.bfloat16), 'dp', axis=0, tiled=True)  39 us
  transfers between devices with their start and end apart: 44, of which 13 were waited for; matrix products, arithmetic and copies ran while one was open for 30% of the time, Pallas kernels for 0%

profile of v2, /device:TPU:0, one launch (start us, length us, event | category | flops | bytes accessed | tf_op | source)
XLA Modules:
  0.0 1393.3 jit_solution(6200642441326243093)
XLA Ops:
  16.3 68.7 %collective-permute-done.1 = bf16[2048,768]{1,0:T(8,128)(2,1)} collective-permute-done((bf16[2048,768]{1,0:T(8,128)(2,1)}, bf16[2048,768]{1,0:T(8,128)(2,1)}, u32[]{:S(2)}, u32[]{:S(2)}) %collective-permute-start.1) | collective-permute-done | bytes 3145760 | tf_op jit(solution)/shard_map/ppermute | solution.py:19
  85.1 66.8 %collective-permute-done.4 = bf16[2048,768]{1,0:T(8,128)(2,1)S(1)} collective-permute-done((bf16[2048,768]{1,0:T(8,128)(2,1)}, bf16[2048,768]{1,0:T(8,128)(2,1)S(1)}, u32[]{:S(2)}, u32[]{:S(2)}) %collective-permute-start.4) | collective-permute-done | bytes 3145760 | tf_op jit(solution)/shard_map/ppermute | solution.py:19
  202.9 31.2 %multiply_convert_fusion.20 = bf16[8192,768]{1,0:T(8,128)(2,1)} fusion(bf16[2048,768]{1,0:T(8,128)(2,1)} %collective-permute-done.5, bf16[2048,768]{1,0:T(8,128)(2,1)S(1)} %collective-permute-done.4, bf16[2048,768]{1,0:T(8,128)(2,1)} %collective-permute-done.3, bf16[2048,768]{1,0:T(8,128)(2,1)S(1)} %copy-done.2, f32[8192]{0:T(1024)S(1)} %pad_maximum_fusion), kind=kLoop, calls=%fused_computation.271 | loop fusion | flops 62914560 | bytes 25198592 | tf_op jit(solution)/shard_map/convert_element_type | solution.py:89
  234.1 108.5 %conditional.3 = (bf16[4096,768]{1,0:T(8,128)(2,1)}, bf16[4096,768]{1,0:T(8,128)(2,1)}, bf16[8,96,3072]{2,1,0:T(8,128)(2,1)}, bf16[8,384,768]{2,1,0:T(8,128)(2,1)}) conditional(s32[]{:T(128)} %clamp.6, (s32[]{:T(128)}, s32[8192]{0:T(1024)S(1)}, bf16[8192,768]{1,0:T(8,128)(2,1)}, bf16[2,768,3072]{2,1,0:T(8,128)(2,1)}, ...), branch_computations={%region_7.8_spmd, %region_8.9_spmd, %region_9.10_spmd, %region_10.... | conditional | flops 116346339328 | bytes 390148320 | solution.py:105
  273.9 11.4 fusion.6
  351.3 79.0 %collective-permute-start.10 = (bf16[384,768]{1,0:T(8,128)(2,1)S(1)}, bf16[384,768]{1,0:T(8,128)(2,1)S(1)}, u32[]{:S(2)}, u32[]{:S(2)}) collective-permute-start(bf16[384,768]{1,0:T(8,128)(2,1)S(1)} %get-tuple-element.428), channel_id=1, source_target_pairs={{0,20},{4,16},{8,28},{12,24},{16,4},{20,0},{24,12},{28,8},{1,21},{... | collective-permute-start | bytes 1769480 | tf_op jit(solution)/shard_map/ppermute | solution.py:51
  439.7 57.4 %collective-permute-start.6 = (bf16[384,768]{1,0:T(8,128)(2,1)S(1)}, bf16[384,768]{1,0:T(8,128)(2,1)S(1)}, u32[]{:S(2)}, u32[]{:S(2)}) collective-permute-start(bf16[384,768]{1,0:T(8,128)(2,1)S(1)} %get-tuple-element.432), channel_id=1, source_target_pairs={{0,4},{4,0},{8,12},{12,8},{16,20},{20,16},{24,28},{28,24},{1,5},{5... | collective-permute-start | bytes 1769480 | tf_op jit(solution)/shard_map/ppermute | solution.py:51
  497.9 35.2 %collective-permute-done.9 = bf16[384,768]{1,0:T(8,128)(2,1)S(1)} collective-permute-done((bf16[384,768]{1,0:T(8,128)(2,1)S(1)}, bf16[384,768]{1,0:T(8,128)(2,1)S(1)}, u32[]{:S(2)}, u32[]{:S(2)}) %collective-permute-start.9) | collective-permute-done | bytes 589856 | tf_op jit(solution)/shard_map/ppermute | solution.py:51
  543.5 13.0 collective-permute-done.18
  556.5 41.7 %collective-permute-start.13 = (bf16[96,3072]{1,0:T(8,128)(2,1)}, bf16[96,3072]{1,0:T(8,128)(2,1)}, u32[]{:S(2)}, u32[]{:S(2)}) collective-permute-start(bf16[96,3072]{1,0:T(8,128)(2,1)} %get-tuple-element.424), channel_id=1, source_target_pairs={{0,4},{4,0},{8,12},{12,8},{16,20},{20,16},{24,28},{28,24},{1,5},{5... | collective-permute-start | bytes 1769480 | tf_op jit(solution)/shard_map/ppermute | solution.py:51
  600.7 201.3 %conditional.4 = (bf16[4096,768]{1,0:T(8,128)(2,1)}, bf16[4096,768]{1,0:T(8,128)(2,1)}, bf16[768,3072]{1,0:T(8,128)(2,1)}, bf16[3072,768]{1,0:T(8,128)(2,1)}) conditional(s32[]{:T(128)} %clamp.7, (s32[4096]{0:T(1024)S(1)}, bf16[8192,768]{1,0:T(8,128)(2,1)}, bf16[768,3072]{1,0:T(8,128)(2,1)}, ...), branch_computations={%region_12.13_spmd, %region_13.14_spmd, %region_14.15_spmd, %regio... | conditional | flops 116341620736 | bytes 401158336
  609.0 16.5 %gather_fusion.11 = bf16[2560,768]{1,0:T(8,128)(2,1)} fusion(bf16[8192,768]{1,0:T(8,128)(2,1)} %get-tuple-element.250, s32[3072]{0:T(1024)S(1)} %pad_clamp_fusion.6), kind=kCustom, calls=%fused_computation.15 | custom fusion | bytes 7874560 | tf_op jit(solution)/shard_map/cond/branch_2_fun/gather | solution.py:26
  625.5 16.5 %gather_fusion.10 = bf16[2560,768]{1,0:T(8,128)(2,1)} fusion(bf16[8192,768]{1,0:T(8,128)(2,1)} %get-tuple-element.245, s32[3072]{0:T(1024)S(1)} %pad_clamp_fusion.6), kind=kCustom, calls=%fused_computation.14 | custom fusion | bytes 7874560 | tf_op jit(solution)/shard_map/cond/branch_2_fun/gather | solution.py:25
  642.1 21.1 %fusion.190 = f32[2560,3072]{1,0:T(8,128)} fusion(bf16[2560,768]{1,0:T(8,128)(2,1)} %gather_fusion.10, bf16[768,3072]{1,0:T(8,128)(2,1)} %get-tuple-element.247), kind=kOutput, calls=%fused_computation.387 | convolution fusion | flops 12079595520 | bytes 40108032 | tf_op jit(solution)/shard_map/cond/branch_2_fun/dot_general | solution.py:27
  663.2 23.1 %convolution_convert_fusion.21 = bf16[2560,768]{1,0:T(8,128)(2,1)S(1)} fusion(bf16[3072,768]{1,0:T(8,128)(2,1)S(1)} %bitcast.285, f32[2560,3072]{1,0:T(8,128)} %fusion.190), kind=kOutput, calls=%fused_computation.225 | convolution fusion | flops 12152340480 | bytes 40108032 | tf_op jit(solution)/shard_map/cond/branch_2_fun/dot_general | solution.py:34
  689.3 26.6 %fusion.141 = bf16[3072,768]{1,0:T(8,128)(2,1)} fusion(bf16[2560,768]{1,0:T(8,128)(2,1)} %gather_fusion.11, pred[2560]{0:T(1024)(128)(4,1)S(1)} %iota_compare_fusion.7, f32[2560,3072]{1,0:T(8,128)} %fusion.190), kind=kOutput, calls=%fused_computation.227 | convolution fusion | flops 12152340480 | bytes 40110592 | tf_op jit(solution)/shard_map/cond/branch_2_fun/kf,kd->fd/dot_general | solution.py:32
  715.8 34.6 %fusion.140 = bf16[2560,3072]{1,0:T(8,128)(2,1)} fusion(f32[2560,3072]{1,0:T(8,128)} %fusion.190, bf16[3072,768]{1,0:T(8,128)(2,1)} %get-tuple-element.248, bf16[2560,768]{1,0:T(8,128)(2,1)} %gather_fusion.11, pred[2560]{0:T(1024)(128)(4,1)S(1)} %iota_compare_fusion.7), kind=kOutput, calls=%fused_computation.222 | convolution fusion | flops 12238848000 | bytes 55839232 | tf_op jit(solution)/shard_map/cond/branch_2_fun/kd,fd->kf/dot_general | solution.py:30
  750.4 15.6 %convolution_convert_fusion.20 = bf16[2560,768]{1,0:T(8,128)(2,1)S(1)} fusion(bf16[2560,3072]{1,0:T(8,128)(2,1)} %fusion.140, bf16[768,3072]{1,0:T(8,128)(2,1)S(1)} %bitcast.275), kind=kOutput, calls=%fused_computation.224 | convolution fusion | flops 12081561600 | bytes 24379392 | tf_op jit(solution)/shard_map/cond/branch_2_fun/kf,df->kd/dot_general | solution.py:35
  766.1 18.2 %fusion.191 = bf16[768,3072]{1,0:T(8,128)(2,1)} fusion(bf16[2560,768]{1,0:T(8,128)(2,1)S(1)} %copy-done.7, bf16[2560,3072]{1,0:T(8,128)(2,1)} %fusion.140), kind=kOutput, calls=%fused_computation.388 | convolution fusion | flops 12079595520 | bytes 24379392 | tf_op jit(solution)/shard_map/cond/branch_2_fun/kd,kf->df/dot_general | solution.py:33
  832.0 25.4 %gather_fusion.23 = bf16[4096,768]{1,0:T(8,128)(2,1)} fusion(bf16[8192,768]{1,0:T(8,128)(2,1)} %constant_dynamic-update-slice_fusion.6, s32[4096]{0:T(1024)S(1)} %broadcast_clamp_fusion), kind=kCustom, calls=%fused_computation.23 | custom fusion | bytes 12599296 | tf_op jit(solution)/shard_map/gather | solution.py:118
  873.4 25.4 %gather_fusion.21 = bf16[4096,768]{1,0:T(8,128)(2,1)} fusion(bf16[8192,768]{1,0:T(8,128)(2,1)} %constant_dynamic-update-slice_fusion.4, s32[4096]{0:T(1024)S(1)} %broadcast_clamp_fusion), kind=kCustom, calls=%fused_computation.21 | custom fusion | bytes 12599296 | tf_op jit(solution)/shard_map/gather | solution.py:118
  909.6 57.4 %collective-permute-done.27 = bf16[384,768]{1,0:T(8,128)(2,1)S(1)} collective-permute-done((bf16[384,768]{1,0:T(8,128)(2,1)S(1)}, bf16[384,768]{1,0:T(8,128)(2,1)S(1)}, u32[]{:S(2)}, u32[]{:S(2)}) %collective-permute-start.27) | collective-permute-done | bytes 589856 | tf_op jit(solution)/shard_map/ppermute | solution.py:51
  982.3 15.4 %collective-permute-done.37 = bf16[96,3072]{1,0:T(8,128)(2,1)S(1)} collective-permute-done((bf16[96,3072]{1,0:T(8,128)(2,1)S(1)}, bf16[96,3072]{1,0:T(8,128)(2,1)S(1)}, u32[]{:S(2)}, u32[]{:S(2)}) %collective-permute-start.37) | collective-permute-done | bytes 589856 | tf_op jit(solution)/shard_map/ppermute | solution.py:51
  999.2 25.3 %gather_fusion.22 = bf16[4096,768]{1,0:T(8,128)(2,1)} fusion(bf16[8192,768]{1,0:T(8,128)(2,1)} %constant_dynamic-update-slice_fusion.6, s32[4096]{0:T(1024)S(1)} %broadcast_clamp_fusion.1), kind=kCustom, calls=%fused_computation.22 | custom fusion | bytes 12599296 | tf_op jit(solution)/shard_map/gather | solution.py:119
  1024.5 25.2 %gather_fusion.20 = bf16[4096,768]{1,0:T(8,128)(2,1)} fusion(bf16[8192,768]{1,0:T(8,128)(2,1)} %constant_dynamic-update-slice_fusion.4, s32[4096]{0:T(1024)S(1)} %broadcast_clamp_fusion.1), kind=kCustom, calls=%fused_computation.20 | custom fusion | bytes 12599296 | tf_op jit(solution)/shard_map/gather | solution.py:119
  1059.5 31.2 %collective-permute-done.35 = bf16[96,3072]{1,0:T(8,128)(2,1)S(1)} collective-permute-done((bf16[96,3072]{1,0:T(8,128)(2,1)}, bf16[96,3072]{1,0:T(8,128)(2,1)S(1)}, u32[]{:S(2)}, u32[]{:S(2)}) %collective-permute-start.35) | collective-permute-done | bytes 589856 | tf_op jit(solution)/shard_map/ppermute | solution.py:51
  1090.8 24.3 %collective-permute-done.34 = bf16[96,3072]{1,0:T(8,128)(2,1)S(1)} collective-permute-done((bf16[96,3072]{1,0:T(8,128)(2,1)}, bf16[96,3072]{1,0:T(8,128)(2,1)S(1)}, u32[]{:S(2)}, u32[]{:S(2)}) %collective-permute-start.34) | collective-permute-done | bytes 589856 | tf_op jit(solution)/shard_map/ppermute | solution.py:51
  1145.7 69.1 %collective-permute-done.38 = bf16[2048,768]{1,0:T(8,128)(2,1)S(1)} collective-permute-done((bf16[2048,768]{1,0:T(8,128)(2,1)}, bf16[2048,768]{1,0:T(8,128)(2,1)S(1)}, u32[]{:S(2)}, u32[]{:S(2)}) %collective-permute-start.38) | collective-permute-done | bytes 3145760 | tf_op jit(solution)/shard_map/ppermute | solution.py:19
  1221.6 92.3 %psum.7 = f32[768,8]{0,1:T(8,128)} all-reduce(f32[768,8]{0,1:T(8,128)S(1)} %convolution_bitcast_fusion), channel_id=1, replica_groups=mesh['dp'=8,'ep'=4] {'dp','ep'}, use_global_device_ids=true, to_apply=%region_18.19 | all-reduce | flops 6144 | bytes 49152 | tf_op jit(solution)/shard_map/psum | solution.py:140
  1323.9 11.8 maximum_convert_fusion.1
  1335.8 39.0 %all-gather.9.cloned.1.call-done = bf16[768,3072]{1,0:T(8,128)(2,1)} async-done(((bf16[96,3072]{1,0:T(8,128)(2,1)}), bf16[768,3072]{1,0:T(8,128)(2,1)}) %all-gather.9.cloned.1.call-update) | async-done | bytes 4718608 | tf_op jit(solution)/shard_map/all_gather | solution.py:58
  1374.7 11.8 maximum_convert_fusion
  (308 shorter events, 283.4 us)
Async XLA Ops:
  7.2 1316.7 %all-gather.11.cloned.1.call-start = ((), (), s32[]{:S(2)}) async-start(), calls=%async_computation.2 | async-start | bytes 5308416 | tf_op jit(solution)/shard_map/all_gather | solution.py:58
  13.7 71.4 %collective-permute-start.1 = (bf16[2048,768]{1,0:T(8,128)(2,1)}, bf16[2048,768]{1,0:T(8,128)(2,1)}, u32[]{:S(2)}, u32[]{:S(2)}) collective-permute-start(bf16[2048,768]{1,0:T(8,128)(2,1)} %param.16), channel_id=1, source_target_pairs={{0,2},{1,3},{2,0},{3,1},{4,6},{5,7},{6,4},{7,5},{8,10},{9,11},{10,... | collective-permute-start | bytes 9437192 | tf_op jit(solution)/shard_map/ppermute | solution.py:19
  15.7 136.2 %collective-permute-start.4 = (bf16[2048,768]{1,0:T(8,128)(2,1)}, bf16[2048,768]{1,0:T(8,128)(2,1)S(1)}, u32[]{:S(2)}, u32[]{:S(2)}) collective-permute-start(bf16[2048,768]{1,0:T(8,128)(2,1)} %param.17), channel_id=1, source_target_pairs={{0,2},{1,3},{2,0},{3,1},{4,6},{5,7},{6,4},{7,5},{8,10},{9,11},{10,... | collective-permute-start | bytes 9437192 | tf_op jit(solution)/shard_map/ppermute | solution.py:19
  15.8 175.7 %collective-permute-start = (bf16[2048,768]{1,0:T(8,128)(2,1)}, bf16[2048,768]{1,0:T(8,128)(2,1)}, u32[]{:S(2)}, u32[]{:S(2)}) collective-permute-start(bf16[2048,768]{1,0:T(8,128)(2,1)} %param.16), channel_id=1, source_target_pairs={{0,1},{1,0},{2,3},{3,2},{4,5},{5,4},{6,7},{7,6},{8,9},{9,8},{10,11... | collective-permute-start | bytes 9437192 | tf_op jit(solution)/shard_map/ppermute | solution.py:19
  15.8 187.1 %collective-permute-start.3 = (bf16[2048,768]{1,0:T(8,128)(2,1)}, bf16[2048,768]{1,0:T(8,128)(2,1)}, u32[]{:S(2)}, u32[]{:S(2)}) collective-permute-start(bf16[2048,768]{1,0:T(8,128)(2,1)} %param.17), channel_id=1, source_target_pairs={{0,1},{1,0},{2,3},{3,2},{4,5},{5,4},{6,7},{7,6},{8,9},{9,8},{10,11... | collective-permute-start | bytes 9437192 | tf_op jit(solution)/shard_map/ppermute | solution.py:19
  85.0 114.2 %collective-permute-start.2 = (bf16[2048,768]{1,0:T(8,128)(2,1)}, bf16[2048,768]{1,0:T(8,128)(2,1)}, u32[]{:S(2)}, u32[]{:S(2)}) collective-permute-start(bf16[2048,768]{1,0:T(8,128)(2,1)} %collective-permute-done.1), channel_id=1, source_target_pairs={{0,1},{1,0},{2,3},{3,2},{4,5},{5,4},{6,7},{7,6},{8,9},{9,8},{10,11... | collective-permute-start | bytes 9437192 | tf_op jit(solution)/shard_map/ppermute | solution.py:19
  346.3 91.9 %collective-permute-start.12 = (bf16[384,768]{1,0:T(8,128)(2,1)S(1)}, bf16[384,768]{1,0:T(8,128)(2,1)S(1)}, u32[]{:S(2)}, u32[]{:S(2)}) collective-permute-start(bf16[384,768]{1,0:T(8,128)(2,1)S(1)} %get-tuple-element.426), channel_id=1, source_target_pairs={{0,28},{4,24},{8,4},{12,0},{16,12},{20,8},{24,20},{28,16},{1,29},{... | collective-permute-start | bytes 1769480 | tf_op jit(solution)/shard_map/ppermute | solution.py:51
  346.3 93.4 %collective-permute-start.11 = (bf16[384,768]{1,0:T(8,128)(2,1)S(1)}, bf16[384,768]{1,0:T(8,128)(2,1)S(1)}, u32[]{:S(2)}, u32[]{:S(2)}) collective-permute-start(bf16[384,768]{1,0:T(8,128)(2,1)S(1)} %get-tuple-element.427), channel_id=1, source_target_pairs={{0,24},{4,28},{8,0},{12,4},{16,8},{20,12},{24,16},{28,20},{1,25},{... | collective-permute-start | bytes 1769480 | tf_op jit(solution)/shard_map/ppermute | solution.py:51
  351.3 146.5 %collective-permute-start.10 = (bf16[384,768]{1,0:T(8,128)(2,1)S(1)}, bf16[384,768]{1,0:T(8,128)(2,1)S(1)}, u32[]{:S(2)}, u32[]{:S(2)}) collective-permute-start(bf16[384,768]{1,0:T(8,128)(2,1)S(1)} %get-tuple-element.428), channel_id=1, source_target_pairs={{0,20},{4,16},{8,28},{12,24},{16,4},{20,0},{24,12},{28,8},{1,21},{... | collective-permute-start | bytes 1769480 | tf_op jit(solution)/shard_map/ppermute | solution.py:51
  430.3 102.7 %collective-permute-start.9 = (bf16[384,768]{1,0:T(8,128)(2,1)S(1)}, bf16[384,768]{1,0:T(8,128)(2,1)S(1)}, u32[]{:S(2)}, u32[]{:S(2)}) collective-permute-start(bf16[384,768]{1,0:T(8,128)(2,1)S(1)} %get-tuple-element.429), channel_id=1, source_target_pairs={{0,16},{4,20},{8,24},{12,28},{16,0},{20,4},{24,8},{28,12},{1,17},{... | collective-permute-start | bytes 1769480 | tf_op jit(solution)/shard_map/ppermute | solution.py:51
  430.9 105.4 %collective-permute-start.8 = (bf16[384,768]{1,0:T(8,128)(2,1)S(1)}, bf16[384,768]{1,0:T(8,128)(2,1)S(1)}, u32[]{:S(2)}, u32[]{:S(2)}) collective-permute-start(bf16[384,768]{1,0:T(8,128)(2,1)S(1)} %get-tuple-element.430), channel_id=1, source_target_pairs={{0,12},{4,8},{8,20},{12,16},{16,28},{20,24},{24,4},{28,0},{1,13},{... | collective-permute-start | bytes 1769480 | tf_op jit(solution)/shard_map/ppermute | solution.py:51
  438.2 98.2 %collective-permute-start.7 = (bf16[384,768]{1,0:T(8,128)(2,1)S(1)}, bf16[384,768]{1,0:T(8,128)(2,1)S(1)}, u32[]{:S(2)}, u32[]{:S(2)}) collective-permute-start(bf16[384,768]{1,0:T(8,128)(2,1)S(1)} %get-tuple-element.431), channel_id=1, source_target_pairs={{0,8},{4,12},{8,16},{12,20},{16,24},{20,28},{24,0},{28,4},{1,9},{5... | collective-permute-start | bytes 1769480 | tf_op jit(solution)/shard_map/ppermute | solution.py:51
  439.7 96.8 %collective-permute-start.6 = (bf16[384,768]{1,0:T(8,128)(2,1)S(1)}, bf16[384,768]{1,0:T(8,128)(2,1)S(1)}, u32[]{:S(2)}, u32[]{:S(2)}) collective-permute-start(bf16[384,768]{1,0:T(8,128)(2,1)S(1)} %get-tuple-element.432), channel_id=1, source_target_pairs={{0,4},{4,0},{8,12},{12,8},{16,20},{20,16},{24,28},{28,24},{1,5},{5... | collective-permute-start | bytes 1769480 | tf_op jit(solution)/shard_map/ppermute | solution.py:51
  536.4 265.7 %collective-permute-start.17 = (bf16[96,3072]{1,0:T(8,128)(2,1)}, bf16[96,3072]{1,0:T(8,128)(2,1)}, u32[]{:S(2)}, u32[]{:S(2)}) collective-permute-start(bf16[96,3072]{1,0:T(8,128)(2,1)} %get-tuple-element.420), channel_id=1, source_target_pairs={{0,20},{4,16},{8,28},{12,24},{16,4},{20,0},{24,12},{28,8},{1,21},{... | collective-permute-start | bytes 1769480 | tf_op jit(solution)/shard_map/ppermute | solution.py:51
  536.4 265.7 %collective-permute-start.16 = (bf16[96,3072]{1,0:T(8,128)(2,1)}, bf16[96,3072]{1,0:T(8,128)(2,1)}, u32[]{:S(2)}, u32[]{:S(2)}) collective-permute-start(bf16[96,3072]{1,0:T(8,128)(2,1)} %get-tuple-element.421), channel_id=1, source_target_pairs={{0,16},{4,20},{8,24},{12,28},{16,0},{20,4},{24,8},{28,12},{1,17},{... | collective-permute-start | bytes 1769480 | tf_op jit(solution)/shard_map/ppermute | solution.py:51
  536.5 265.6 %collective-permute-start.15 = (bf16[96,3072]{1,0:T(8,128)(2,1)}, bf16[96,3072]{1,0:T(8,128)(2,1)}, u32[]{:S(2)}, u32[]{:S(2)}) collective-permute-start(bf16[96,3072]{1,0:T(8,128)(2,1)} %get-tuple-element.422), channel_id=1, source_target_pairs={{0,12},{4,8},{8,20},{12,16},{16,28},{20,24},{24,4},{28,0},{1,13},{... | collective-permute-start | bytes 1769480 | tf_op jit(solution)/shard_map/ppermute | solution.py:51
  542.2 259.9 %collective-permute-start.14 = (bf16[96,3072]{1,0:T(8,128)(2,1)}, bf16[96,3072]{1,0:T(8,128)(2,1)}, u32[]{:S(2)}, u32[]{:S(2)}) collective-permute-start(bf16[96,3072]{1,0:T(8,128)(2,1)} %get-tuple-element.423), channel_id=1, source_target_pairs={{0,8},{4,12},{8,16},{12,20},{16,24},{20,28},{24,0},{28,4},{1,9},{5... | collective-permute-start | bytes 1769480 | tf_op jit(solution)/shard_map/ppermute | solution.py:51
  556.5 245.6 %collective-permute-start.13 = (bf16[96,3072]{1,0:T(8,128)(2,1)}, bf16[96,3072]{1,0:T(8,128)(2,1)}, u32[]{:S(2)}, u32[]{:S(2)}) collective-permute-start(bf16[96,3072]{1,0:T(8,128)(2,1)} %get-tuple-element.424), channel_id=1, source_target_pairs={{0,4},{4,0},{8,12},{12,8},{16,20},{20,16},{24,28},{28,24},{1,5},{5... | collective-permute-start | bytes 1769480 | tf_op jit(solution)/shard_map/ppermute | solution.py:51
  805.8 518.1 %all-gather.13.cloned.1.call-start = ((), (), s32[]{:S(2)}) async-start(), calls=%async_computation.3 | async-start | bytes 5308416 | tf_op jit(solution)/shard_map/all_gather | solution.py:58
  821.7 83.4 %collective-permute-start.30 = (bf16[384,768]{1,0:T(8,128)(2,1)}, bf16[384,768]{1,0:T(8,128)(2,1)}, u32[]{:S(2)}, u32[]{:S(2)}) collective-permute-start(bf16[384,768]{1,0:T(8,128)(2,1)} %get-tuple-element.410), channel_id=1, source_target_pairs={{0,28},{4,24},{8,4},{12,0},{16,12},{20,8},{24,20},{28,16},{1,29},{... | collective-permute-start | bytes 1769480 | tf_op jit(solution)/shard_map/ppermute | solution.py:51
  821.7 84.0 %collective-permute-start.29 = (bf16[384,768]{1,0:T(8,128)(2,1)}, bf16[384,768]{1,0:T(8,128)(2,1)}, u32[]{:S(2)}, u32[]{:S(2)}) collective-permute-start(bf16[384,768]{1,0:T(8,128)(2,1)} %get-tuple-element.411), channel_id=1, source_target_pairs={{0,24},{4,28},{8,0},{12,4},{16,8},{20,12},{24,16},{28,20},{1,25},{... | collective-permute-start | bytes 1769480 | tf_op jit(solution)/shard_map/ppermute | solution.py:51
  821.8 86.1 %collective-permute-start.28 = (bf16[384,768]{1,0:T(8,128)(2,1)}, bf16[384,768]{1,0:T(8,128)(2,1)}, u32[]{:S(2)}, u32[]{:S(2)}) collective-permute-start(bf16[384,768]{1,0:T(8,128)(2,1)} %get-tuple-element.412), channel_id=1, source_target_pairs={{0,20},{4,16},{8,28},{12,24},{16,4},{20,0},{24,12},{28,8},{1,21},{... | collective-permute-start | bytes 1769480 | tf_op jit(solution)/shard_map/ppermute | solution.py:51
  862.3 187.6 %collective-permute-start.22 = (bf16[2048,768]{1,0:T(8,128)(2,1)}, bf16[2048,768]{1,0:T(8,128)(2,1)}, u32[]{:S(2)}, u32[]{:S(2)}) collective-permute-start(bf16[2048,768]{1,0:T(8,128)(2,1)} %get-tuple-element.395), channel_id=1, source_target_pairs={{0,1},{1,0},{2,3},{3,2},{4,5},{5,4},{6,7},{7,6},{8,9},{9,8},{10,11... | collective-permute-start | bytes 9437192 | tf_op jit(solution)/shard_map/ppermute | solution.py:19
  904.9 210.2 %collective-permute-start.20 = (bf16[2048,768]{1,0:T(8,128)(2,1)}, bf16[2048,768]{1,0:T(8,128)(2,1)}, u32[]{:S(2)}, u32[]{:S(2)}) collective-permute-start(bf16[2048,768]{1,0:T(8,128)(2,1)} %get-tuple-element.399), channel_id=1, source_target_pairs={{0,1},{1,0},{2,3},{3,2},{4,5},{5,4},{6,7},{7,6},{8,9},{9,8},{10,11... | collective-permute-start | bytes 9437192 | tf_op jit(solution)/shard_map/ppermute | solution.py:19
  905.1 61.8 %collective-permute-start.27 = (bf16[384,768]{1,0:T(8,128)(2,1)S(1)}, bf16[384,768]{1,0:T(8,128)(2,1)S(1)}, u32[]{:S(2)}, u32[]{:S(2)}) collective-permute-start(bf16[384,768]{1,0:T(8,128)(2,1)S(1)} %copy-done.19), channel_id=1, source_target_pairs={{0,16},{4,20},{8,24},{12,28},{16,0},{20,4},{24,8},{28,12},{1,17},{... | collective-permute-start | bytes 1769480 | tf_op jit(solution)/shard_map/ppermute | solution.py:51
  967.5 164.7 %collective-permute-start.23 = (bf16[2048,768]{1,0:T(8,128)(2,1)S(1)}, bf16[2048,768]{1,0:T(8,128)(2,1)}, u32[]{:S(2)}, u32[]{:S(2)}) collective-permute-start(bf16[2048,768]{1,0:T(8,128)(2,1)S(1)} %get-tuple-element.394), channel_id=1, source_target_pairs={{0,1},{1,0},{2,3},{3,2},{4,5},{5,4},{6,7},{7,6},{8,9},{9,8},{10,11... | collective-permute-start | bytes 9437192 | tf_op jit(solution)/shard_map/ppermute | solution.py:19
  967.6 164.6 %collective-permute-start.21 = (bf16[2048,768]{1,0:T(8,128)(2,1)}, bf16[2048,768]{1,0:T(8,128)(2,1)}, u32[]{:S(2)}, u32[]{:S(2)}) collective-permute-start(bf16[2048,768]{1,0:T(8,128)(2,1)} %get-tuple-element.398), channel_id=1, source_target_pairs={{0,1},{1,0},{2,3},{3,2},{4,5},{5,4},{6,7},{7,6},{8,9},{9,8},{10,11... | collective-permute-start | bytes 9437192 | tf_op jit(solution)/shard_map/ppermute | solution.py:19
  1049.9 65.3 %collective-permute-start.34 = (bf16[96,3072]{1,0:T(8,128)(2,1)}, bf16[96,3072]{1,0:T(8,128)(2,1)S(1)}, u32[]{:S(2)}, u32[]{:S(2)}) collective-permute-start(bf16[96,3072]{1,0:T(8,128)(2,1)} %get-tuple-element.405), channel_id=1, source_target_pairs={{0,16},{4,20},{8,24},{12,28},{16,0},{20,4},{24,8},{28,12},{1,17},{... | collective-permute-start | bytes 1769480 | tf_op jit(solution)/shard_map/ppermute | solution.py:51
  1136.3 199.5 %all-gather.7.cloned.1.call-start = ((), (), s32[]{:S(2)}) async-start(), calls=%async_computation | async-start | bytes 5308416 | tf_op jit(solution)/shard_map/all_gather | solution.py:58
  1140.3 234.4 %all-gather.9.cloned.1.call-start = ((), (), s32[]{:S(2)}) async-start(), calls=%async_computation.1 | async-start | bytes 5308416 | tf_op jit(solution)/shard_map/all_gather | solution.py:58
  1143.6 71.2 %collective-permute-start.38 = (bf16[2048,768]{1,0:T(8,128)(2,1)}, bf16[2048,768]{1,0:T(8,128)(2,1)S(1)}, u32[]{:S(2)}, u32[]{:S(2)}) collective-permute-start(bf16[2048,768]{1,0:T(8,128)(2,1)} %get-tuple-element.346), channel_id=1, source_target_pairs={{0,2},{1,3},{2,0},{3,1},{4,6},{5,7},{6,4},{7,5},{8,10},{9,11},{10,... | collective-permute-start | bytes 9437192 | tf_op jit(solution)/shard_map/ppermute | solution.py:19
  1143.7 174.4 %collective-permute-start.39 = (bf16[2048,768]{1,0:T(8,128)(2,1)}, bf16[2048,768]{1,0:T(8,128)(2,1)}, u32[]{:S(2)}, u32[]{:S(2)}) collective-permute-start(bf16[2048,768]{1,0:T(8,128)(2,1)} %get-tuple-element.349), channel_id=1, source_target_pairs={{0,2},{1,3},{2,0},{3,1},{4,6},{5,7},{6,4},{7,5},{8,10},{9,11},{10,... | collective-permute-start | bytes 9437192 | tf_op jit(solution)/shard_map/ppermute | solution.py:19
  (87 other events, 4539.4 us)
Sparse Core Ops, SparseCore 0:
  806.0 153.3 all-gather.10
  1136.4 77.4 all-gather.12
  1216.1 78.5 all-gather.6
  1297.3 77.4 all-gather.8
